TPU v7x, 32 devices: a 4x4x1 block of a 4x4x8 slice. The times are simulated.
32 devices in a mesh: dp: 1 (over z), tp: 4 (over y), cp: 8 (over x, core).
Axes of the slice: x: 4, y: 4, z: 1, core: 2. Of those that a mesh axis runs over, the one named last changes fastest.
The devices are a block of a 4x4x8 slice.
Arguments:
- hidden: bfloat16 [2048, 5120], P(('dp', 'cp'))
- positions: int32 [2048], P(('dp', 'cp'))
- norm_gain: bfloat16 [5120], replicated
- w_query: bfloat16 [5120, 4096], P(None, 'tp')
- w_key: bfloat16 [5120, 1024], P(None, 'tp')
- w_value: bfloat16 [5120, 1024], P(None, 'tp')
- w_out: bfloat16 [4096, 5120], P('tp')
Outputs:
- output 1: bfloat16 [2048, 5120], P(('dp', 'cp'))
- output 2: bfloat16 [2048, 8, 128], P(('dp', 'cp'), 'tp')
- output 3: bfloat16 [2048, 8, 128], P(('dp', 'cp'), 'tp')
All inputs are finite; a program needn't handle non-finite values.
Results may differ from a plain program's by a relative error of at most 0.00862386.
Values are sent between devices in bfloat16 or wider.
A program may use at most 768 MiB of HBM per device.

v0:
```python
import math
import jax
import jax.numpy as jnp
from jax import lax
from jax.sharding import PartitionSpec as P

HEAD = 128
EPS = 1e-5
LOG_THETA = math.log(1000000.0)
SCORE_SCALE = 1.0 / math.sqrt(HEAD)


def rms_norm(hidden, norm_gain):
    hidden_f = hidden.astype(jnp.float32)
    inv_rms = lax.rsqrt(jnp.mean(hidden_f * hidden_f, axis=-1, keepdims=True) + EPS)
    return (hidden_f * inv_rms * norm_gain.astype(jnp.float32)).astype(jnp.bfloat16)


def rope_tables(positions):
    half_dim = HEAD // 2
    inv_freq = jnp.exp(jnp.arange(half_dim, dtype=jnp.float32) * (-2.0 * LOG_THETA / HEAD))
    angles = positions.astype(jnp.float32)[..., None] * inv_freq
    return jnp.cos(angles), jnp.sin(angles)


def apply_rope(head_vals, cos_t, sin_t):
    half_dim = HEAD // 2
    first_half = head_vals[..., :half_dim]
    second_half = head_vals[..., half_dim:]
    return jnp.concatenate([first_half * cos_t - second_half * sin_t, second_half * cos_t + first_half * sin_t], axis=-1)


def project_heads(hidden, positions, norm_gain, w_query, w_key, w_value):
    row_count = hidden.shape[0]
    kv_local = w_key.shape[1] // HEAD
    group_size = w_query.shape[1] // (HEAD * kv_local)
    normed = rms_norm(hidden, norm_gain)
    cos_t, sin_t = rope_tables(positions)
    q_proj = jnp.dot(normed, w_query, preferred_element_type=jnp.float32).reshape(row_count, kv_local, group_size, HEAD)
    queries = apply_rope(q_proj, cos_t[:, None, None, :], sin_t[:, None, None, :]).astype(jnp.bfloat16)
    k_proj = jnp.dot(normed, w_key, preferred_element_type=jnp.float32).reshape(row_count, kv_local, HEAD)
    k_rope = apply_rope(k_proj, cos_t[:, None, :], sin_t[:, None, :]).astype(jnp.bfloat16)
    v_heads = jnp.dot(normed, w_value, preferred_element_type=jnp.float32).astype(jnp.bfloat16).reshape(row_count, kv_local, HEAD)
    return queries, k_rope, v_heads


def own_block_stats(queries, k_rope, v_heads, positions):
    scores = jnp.einsum('uohf,tof->ohut', queries, k_rope, preferred_element_type=jnp.float32) * SCORE_SCALE
    visible = positions[None, :] <= positions[:, None]
    scores = jnp.where(visible, scores, -jnp.inf)
    run_max = jnp.max(scores, axis=-1)
    weights = jnp.exp(scores - run_max[..., None])
    run_sum = jnp.sum(weights, axis=-1)
    acc_out = jnp.einsum('ohut,tof->ohuf', weights.astype(jnp.bfloat16), v_heads, preferred_element_type=jnp.float32)
    return run_max, run_sum, acc_out


def attend_block(queries, kv_blk, soft_stats):
    run_max, run_sum, acc_out = soft_stats
    scores = jnp.einsum('uohf,tof->ohut', queries, kv_blk[0], preferred_element_type=jnp.float32) * SCORE_SCALE
    new_max = jnp.maximum(run_max, jnp.max(scores, axis=-1))
    rescale = jnp.exp(run_max - new_max)
    weights = jnp.exp(scores - new_max[..., None])
    new_sum = run_sum * rescale + jnp.sum(weights, axis=-1)
    new_acc = acc_out * rescale[..., None] + jnp.einsum('ohut,tof->ohuf', weights.astype(jnp.bfloat16), kv_blk[1], preferred_element_type=jnp.float32)
    return new_max, new_sum, new_acc


def output_sum(hidden, soft_stats, w_out):
    run_max, run_sum, acc_out = soft_stats
    attn_o = (acc_out / run_sum[..., None]).astype(jnp.bfloat16)
    w_out_r = w_out.reshape(acc_out.shape[0], acc_out.shape[1], HEAD, hidden.shape[1])
    part_sum = jnp.einsum('ngte,ngef->tf', attn_o, w_out_r, preferred_element_type=jnp.float32).astype(jnp.bfloat16)
    attn_sum = lax.psum(part_sum, 'tp')
    return (hidden.astype(jnp.float32) + attn_sum.astype(jnp.float32)).astype(jnp.bfloat16)


def solution(mesh):
    blocks = mesh.shape['cp']
    shift_pairs = [(src_idx, (src_idx + 1) % blocks) for src_idx in range(blocks)]
    row_spec = P(('dp', 'cp'), None)
    cache_spec = P(('dp', 'cp'), 'tp', None)
    head_cols = P(None, 'tp')

    def local_block(hidden, positions, norm_gain, w_query, w_key, w_value, w_out):
        my_block = lax.axis_index('cp')
        queries, k_rope, v_heads = project_heads(hidden, positions, norm_gain, w_query, w_key, w_value)
        soft_stats = own_block_stats(queries, k_rope, v_heads, positions)

        def shift_step(step_idx, loop_carry):
            kv_blk, stats_in = loop_carry
            kv_blk = lax.ppermute(kv_blk, 'cp', shift_pairs)

            def take_block(state_in):
                return attend_block(queries, kv_blk, state_in)

            def keep_stats(state_in):
                return state_in

            stats_out = lax.cond(step_idx <= my_block, take_block, keep_stats, stats_in)
            return kv_blk, stats_out

        kv_own = jnp.stack([k_rope, v_heads])
        _, soft_stats = lax.fori_loop(1, blocks, shift_step, (kv_own, soft_stats))
        return output_sum(hidden, soft_stats, w_out), k_rope, v_heads

    return jax.shard_map(local_block, mesh=mesh, in_specs=(row_spec, P(('dp', 'cp')), P(None), head_cols, head_cols, head_cols, P('tp', None)), out_specs=(row_spec, cache_spec, cache_spec), check_vma=False)
```

profile of v0, /device:TPU:102, one launch (start us, length us, event | category | flops | bytes accessed | tf_op | source)
XLA Modules:
  0.0 186.3 jit_solution(13505968092168666882)
XLA Ops:
  7.3 0.8 convert_element_type.53
  8.1 1.9 %broadcast_compare_fusion = pred[256,256]{0,1:T(8,128)(4,1)} fusion(s32[256]{0:T(256)} %param.12), kind=kLoop, calls=%fused_computation.46 | loop fusion | flops 65536 | bytes 66560 | tf_op jit(solution)/shard_map/le | solution.py:49
  10.0 0.7 convert_element_type.51
  10.7 2.3 %fusion.20 = f32[256]{0:T(256)S(1)} fusion(bf16[256,5120]{1,0:T(8,128)(2,1)} %param.11), kind=kLoop, calls=%fused_computation.23 | loop fusion | flops 3931904 | bytes 2622464 | tf_op jit(solution)/shard_map/reduce_sum | solution.py:15
  13.1 1.4 fusion.34
  14.7 8.7 %fusion.31 = f32[256,1024]{1,0:T(8,128)} fusion(bf16[5120,1024]{1,0:T(8,128)(2,1)} %param.14, bf16[256,5120]{1,0:T(8,128)(2,1)} %param.11, f32[5120]{0:T(1024)S(1)} %convert_element_type.51, f32[256]{0:T(256)S(1)} %add_rsqrt_fusion), kind=kOutput, calls=%fused_computation.49 | convolution fusion | flops 2689597440 | bytes 14177280 | tf_op jit(solution)/shard_map/dot_general | solution.py:39
  23.4 2.7 %reshape.158 = f32[256,2,4,128]{3,2,1,0:T(4,128)} reshape(f32[256,1024]{1,0:T(8,128)} %fusion.31) | data formatting | bytes 2097152 | tf_op jit(solution)/shard_map/reshape | solution.py:39
  26.1 2.4 %fusion.36 = (f32[256,2,4,64]{3,2,1,0:T(4,128)S(1)}, f32[256,2,4,64]{3,2,1,0:T(4,128)S(1)}) fusion(f32[256,2,4,128]{3,2,1,0:T(4,128)} %reshape.158), kind=kLoop, calls=%fused_computation.51 | loop fusion | bytes 2097152 | tf_op jit(solution)/shard_map/slice | solution.py:28
  28.5 3.1 %convolution_convert_fusion = bf16[256,256]{0,1:T(8,128)(2,1)S(1)} fusion(bf16[5120,256]{1,0:T(8,128)(2,1)} %param.16, bf16[256,5120]{1,0:T(8,128)(2,1)S(1)} %copy-done.4, f32[5120]{0:T(1024)S(1)} %convert_element_type.51, f32[256]{0:T(256)S(1)} %add_rsqrt_fusion), kind=kOutput, calls=%fused_computation.31 | convolution fusion | flops 676397056 | bytes 5395456 | tf_op jit(solution)/shard_map/dot_general | solution.py:43
  34.4 1.5 fusion.26
  36.0 0.8 copy.13
  36.7 1.8 pad_maximum_fusion.1
  38.5 64.2 %while.19 = (s32[]{:T(128)}, bf16[2,256,2,128]{3,1,2,0:T(8,128)(2,1)}, f32[2,4,256]{2,1,0:T(4,128)S(1)}, f32[2,4,256]{2,1,0:T(4,128)S(1)}, f32[2,4,256,128]{3,2,...) while((s32[]{:T(128)}, bf16[2,256,2,128]{3,1,2,0:T(8,128)(2,1)}, ...), condition=%wide.region_8.9_spmd, body=%wide.region_3.8_spmd.sunk | while | flops 273158144 | bytes 19267876 | solution.py:104
  38.5 5.8 %collective-permute-done = bf16[2,256,2,128]{3,1,2,0:T(8,128)(2,1)S(1)} collective-permute-done((bf16[2,256,2,128]{3,1,2,0:T(8,128)(2,1)}, bf16[2,256,2,128]{3,1,2,0:T(8,128)(2,1)S(1)}, u32[]{:S(2)}, u32[]{:S(2)}) %collective-permute-start) | collective-permute-done | bytes 262176 | tf_op jit(solution)/shard_map/while/body/eval_jaxpr/ppermute | solution.py:92
  44.3 3.1 %conditional.2 = ((f32[2,4,256]{2,1,0:T(4,128)S(1)}, f32[2,4,256]{2,1,0:T(4,128)S(1)}, f32[2,4,256,128]{3,2,1,0:T(8,128)})) conditional(s32[]{:T(128)} %convert_element_type.90, (f32[2,4,256]{2,1,0:T(4,128)S(1)}, f32[2,4,256]{2,1,0:T(4,128)S(1)}, f32[2,4,256,128]{3,2,1,0:T(8,128)}) %tuple.51, (bf16[2,256,2,128]{3,1,2,0:T(8,128)(2,1)S(1)}, ...), branch_computations={%region_4.4_spmd, %region_5.7_spmd} | conditional | flops 273158144 | bytes 17694808 | solution.py:100
  45.5 0.9 convolution_add_fusion
  46.5 1.0 copy-done.2
  47.4 0.7 copy.64
  48.1 5.8 %collective-permute-done = bf16[2,256,2,128]{3,1,2,0:T(8,128)(2,1)S(1)} collective-permute-done((bf16[2,256,2,128]{3,1,2,0:T(8,128)(2,1)}, bf16[2,256,2,128]{3,1,2,0:T(8,128)(2,1)S(1)}, u32[]{:S(2)}, u32[]{:S(2)}) %collective-permute-start) | collective-permute-done | bytes 262176 | tf_op jit(solution)/shard_map/while/body/eval_jaxpr/ppermute | solution.py:92
  53.9 3.1 %conditional.2 = ((f32[2,4,256]{2,1,0:T(4,128)S(1)}, f32[2,4,256]{2,1,0:T(4,128)S(1)}, f32[2,4,256,128]{3,2,1,0:T(8,128)})) conditional(s32[]{:T(128)} %convert_element_type.90, (f32[2,4,256]{2,1,0:T(4,128)S(1)}, f32[2,4,256]{2,1,0:T(4,128)S(1)}, f32[2,4,256,128]{3,2,1,0:T(8,128)}) %tuple.51, (bf16[2,256,2,128]{3,1,2,0:T(8,128)(2,1)S(1)}, ...), branch_computations={%region_4.4_spmd, %region_5.7_spmd} | conditional | flops 273158144 | bytes 17694808 | solution.py:100
  55.1 0.9 convolution_add_fusion
  56.1 1.0 copy-done.2
  57.0 0.7 copy.64
  57.7 5.8 %collective-permute-done = bf16[2,256,2,128]{3,1,2,0:T(8,128)(2,1)S(1)} collective-permute-done((bf16[2,256,2,128]{3,1,2,0:T(8,128)(2,1)}, bf16[2,256,2,128]{3,1,2,0:T(8,128)(2,1)S(1)}, u32[]{:S(2)}, u32[]{:S(2)}) %collective-permute-start) | collective-permute-done | bytes 262176 | tf_op jit(solution)/shard_map/while/body/eval_jaxpr/ppermute | solution.py:92
  63.5 3.1 %conditional.2 = ((f32[2,4,256]{2,1,0:T(4,128)S(1)}, f32[2,4,256]{2,1,0:T(4,128)S(1)}, f32[2,4,256,128]{3,2,1,0:T(8,128)})) conditional(s32[]{:T(128)} %convert_element_type.90, (f32[2,4,256]{2,1,0:T(4,128)S(1)}, f32[2,4,256]{2,1,0:T(4,128)S(1)}, f32[2,4,256,128]{3,2,1,0:T(8,128)}) %tuple.51, (bf16[2,256,2,128]{3,1,2,0:T(8,128)(2,1)S(1)}, ...), branch_computations={%region_4.4_spmd, %region_5.7_spmd} | conditional | flops 273158144 | bytes 17694808 | solution.py:100
  64.8 0.9 convolution_add_fusion
  65.7 1.0 copy-done.2
  66.6 0.7 copy.64
  67.4 5.8 %collective-permute-done = bf16[2,256,2,128]{3,1,2,0:T(8,128)(2,1)S(1)} collective-permute-done((bf16[2,256,2,128]{3,1,2,0:T(8,128)(2,1)}, bf16[2,256,2,128]{3,1,2,0:T(8,128)(2,1)S(1)}, u32[]{:S(2)}, u32[]{:S(2)}) %collective-permute-start) | collective-permute-done | bytes 262176 | tf_op jit(solution)/shard_map/while/body/eval_jaxpr/ppermute | solution.py:92
  73.1 3.1 %conditional.2 = ((f32[2,4,256]{2,1,0:T(4,128)S(1)}, f32[2,4,256]{2,1,0:T(4,128)S(1)}, f32[2,4,256,128]{3,2,1,0:T(8,128)})) conditional(s32[]{:T(128)} %convert_element_type.90, (f32[2,4,256]{2,1,0:T(4,128)S(1)}, f32[2,4,256]{2,1,0:T(4,128)S(1)}, f32[2,4,256,128]{3,2,1,0:T(8,128)}) %tuple.51, (bf16[2,256,2,128]{3,1,2,0:T(8,128)(2,1)S(1)}, ...), branch_computations={%region_4.4_spmd, %region_5.7_spmd} | conditional | flops 273158144 | bytes 17694808 | solution.py:100
  74.4 0.9 convolution_add_fusion
  75.3 1.0 copy-done.2
  76.3 0.7 copy.64
  77.0 5.8 %collective-permute-done = bf16[2,256,2,128]{3,1,2,0:T(8,128)(2,1)S(1)} collective-permute-done((bf16[2,256,2,128]{3,1,2,0:T(8,128)(2,1)}, bf16[2,256,2,128]{3,1,2,0:T(8,128)(2,1)S(1)}, u32[]{:S(2)}, u32[]{:S(2)}) %collective-permute-start) | collective-permute-done | bytes 262176 | tf_op jit(solution)/shard_map/while/body/eval_jaxpr/ppermute | solution.py:92
  82.8 3.1 %conditional.2 = ((f32[2,4,256]{2,1,0:T(4,128)S(1)}, f32[2,4,256]{2,1,0:T(4,128)S(1)}, f32[2,4,256,128]{3,2,1,0:T(8,128)})) conditional(s32[]{:T(128)} %convert_element_type.90, (f32[2,4,256]{2,1,0:T(4,128)S(1)}, f32[2,4,256]{2,1,0:T(4,128)S(1)}, f32[2,4,256,128]{3,2,1,0:T(8,128)}) %tuple.51, (bf16[2,256,2,128]{3,1,2,0:T(8,128)(2,1)S(1)}, ...), branch_computations={%region_4.4_spmd, %region_5.7_spmd} | conditional | flops 273158144 | bytes 17694808 | solution.py:100
  84.0 0.9 convolution_add_fusion
  84.9 1.0 copy-done.2
  86.6 5.8 %collective-permute-done = bf16[2,256,2,128]{3,1,2,0:T(8,128)(2,1)S(1)} collective-permute-done((bf16[2,256,2,128]{3,1,2,0:T(8,128)(2,1)}, bf16[2,256,2,128]{3,1,2,0:T(8,128)(2,1)S(1)}, u32[]{:S(2)}, u32[]{:S(2)}) %collective-permute-start) | collective-permute-done | bytes 262176 | tf_op jit(solution)/shard_map/while/body/eval_jaxpr/ppermute | solution.py:92
  92.4 3.1 %conditional.2 = ((f32[2,4,256]{2,1,0:T(4,128)S(1)}, f32[2,4,256]{2,1,0:T(4,128)S(1)}, f32[2,4,256,128]{3,2,1,0:T(8,128)})) conditional(s32[]{:T(128)} %convert_element_type.90, (f32[2,4,256]{2,1,0:T(4,128)S(1)}, f32[2,4,256]{2,1,0:T(4,128)S(1)}, f32[2,4,256,128]{3,2,1,0:T(8,128)}) %tuple.51, (bf16[2,256,2,128]{3,1,2,0:T(8,128)(2,1)S(1)}, ...), branch_computations={%region_4.4_spmd, %region_5.7_spmd} | conditional | flops 273158144 | bytes 17694808 | solution.py:100
  93.6 0.9 convolution_add_fusion
  94.5 1.0 copy-done.2
  96.2 5.8 %collective-permute-done = bf16[2,256,2,128]{3,1,2,0:T(8,128)(2,1)S(1)} collective-permute-done((bf16[2,256,2,128]{3,1,2,0:T(8,128)(2,1)}, bf16[2,256,2,128]{3,1,2,0:T(8,128)(2,1)S(1)}, u32[]{:S(2)}, u32[]{:S(2)}) %collective-permute-start) | collective-permute-done | bytes 262176 | tf_op jit(solution)/shard_map/while/body/eval_jaxpr/ppermute | solution.py:92
  102.0 0.7 copy.64
  102.7 7.0 %fusion.17 = bf16[256,5120]{1,0:T(8,128)(2,1)} fusion(bf16[2,4,128,5120]{3,2,1,0:T(8,128)(2,1)} %bitcast.73, f32[2,4,256,128]{3,2,1,0:T(8,128)} %get-tuple-element.158, f32[2,4,256]{2,1,0:T(4,128)S(1)} %get-tuple-element.159), kind=kOutput, calls=%fused_computation.22 | convolution fusion | flops 2686189568 | bytes 14163968 | tf_op jit(solution)/shard_map/ngte,ngef->tf/dot_general | solution.py:73
  109.8 0.8 copy.20
  110.6 0.8 copy.21
  111.4 63.1 %all-reduce.2.cloned.1.call-done = bf16[256,5120]{1,0:T(8,128)(2,1)} async-done(((bf16[256,5120]{1,0:T(8,128)(2,1)}), bf16[256,5120]{1,0:T(8,128)(2,1)}) %all-reduce.2.cloned.1.call-update) | async-done | bytes 2621456 | tf_op jit(solution)/shard_map/psum | solution.py:74
  174.5 5.0 %fusion.23 = bf16[256,5120]{1,0:T(8,128)(2,1)} fusion(bf16[256,5120]{1,0:T(8,128)(2,1)} %param.11, bf16[256,5120]{1,0:T(8,128)(2,1)} %all-reduce.2.cloned.1.call-done), kind=kLoop, calls=%fused_computation.26 | loop fusion | flops 5242880 | bytes 7864320 | tf_op jit(solution)/shard_map/convert_element_type | solution.py:75
  (86 shorter events, 11.9 us)
Async XLA Ops:
  7.2 5.9 %copy-start = (bf16[5120,256]{1,0:T(8,128)(2,1)S(1)}, bf16[5120,256]{1,0:T(8,128)(2,1)}, u32[]{:S(2)}) copy-start(bf16[5120,256]{1,0:T(8,128)(2,1)} %param.15) | copy-start | bytes 7864324
  7.2 167.3 %all-reduce.2.cloned.1.call-start = ((), (), s32[]{:S(2)}) async-start(), calls=%async_computation | async-start | bytes 5242880 | tf_op jit(solution)/shard_map/psum | solution.py:74
  7.3 5.8 %copy-start.3 = (bf16[256,5120]{1,0:T(8,128)(2,1)S(1)}, bf16[256,5120]{1,0:T(8,128)(2,1)}, u32[]{:S(2)}) copy-start(bf16[256,5120]{1,0:T(8,128)(2,1)} %param.11) | copy-start | bytes 7864324
  26.1 2.4 %copy-start.4 = (bf16[256,5120]{1,0:T(8,128)(2,1)S(1)}, bf16[256,5120]{1,0:T(8,128)(2,1)}, u32[]{:S(2)}) copy-start(bf16[256,5120]{1,0:T(8,128)(2,1)} %param.11) | copy-start | bytes 7864324
  31.6 4.3 %copy-start.5 = (bf16[256,256]{0,1:T(8,128)(2,1)}, bf16[256,256]{0,1:T(8,128)(2,1)S(1)}, u32[]{:S(2)}) copy-start(bf16[256,256]{0,1:T(8,128)(2,1)S(1)} %convolution_convert_fusion) | copy-start | bytes 393220
  32.3 0.7 copy-start.7
  32.3 1.4 copy-start.8
  38.5 5.8 %collective-permute-start = (bf16[2,256,2,128]{3,1,2,0:T(8,128)(2,1)}, bf16[2,256,2,128]{3,1,2,0:T(8,128)(2,1)S(1)}, u32[]{:S(2)}, u32[]{:S(2)}) collective-permute-start(bf16[2,256,2,128]{3,1,2,0:T(8,128)(2,1)} %get-tuple-element.259), channel_id=1, source_target_pairs={{0,1},{1,2},{2,3},{3,4},{4,5},{5,6},{6,7},{7,0},{8,9},{9,10},{10,1... | collective-permute-start | bytes 786440 | tf_op jit(solution)/shard_map/while/body/eval_jaxpr/ppermute | solution.py:92
  44.3 1.2 copy-start.1
  46.4 1.0 copy-start.2
  48.1 5.8 %collective-permute-start = (bf16[2,256,2,128]{3,1,2,0:T(8,128)(2,1)}, bf16[2,256,2,128]{3,1,2,0:T(8,128)(2,1)S(1)}, u32[]{:S(2)}, u32[]{:S(2)}) collective-permute-start(bf16[2,256,2,128]{3,1,2,0:T(8,128)(2,1)} %get-tuple-element.259), channel_id=1, source_target_pairs={{0,1},{1,2},{2,3},{3,4},{4,5},{5,6},{6,7},{7,0},{8,9},{9,10},{10,1... | collective-permute-start | bytes 786440 | tf_op jit(solution)/shard_map/while/body/eval_jaxpr/ppermute | solution.py:92
  53.9 1.2 copy-start.1
  56.1 1.0 copy-start.2
  57.7 5.8 %collective-permute-start = (bf16[2,256,2,128]{3,1,2,0:T(8,128)(2,1)}, bf16[2,256,2,128]{3,1,2,0:T(8,128)(2,1)S(1)}, u32[]{:S(2)}, u32[]{:S(2)}) collective-permute-start(bf16[2,256,2,128]{3,1,2,0:T(8,128)(2,1)} %get-tuple-element.259), channel_id=1, source_target_pairs={{0,1},{1,2},{2,3},{3,4},{4,5},{5,6},{6,7},{7,0},{8,9},{9,10},{10,1... | collective-permute-start | bytes 786440 | tf_op jit(solution)/shard_map/while/body/eval_jaxpr/ppermute | solution.py:92
  63.5 1.2 copy-start.1
  65.7 1.0 copy-start.2
  67.3 5.8 %collective-permute-start = (bf16[2,256,2,128]{3,1,2,0:T(8,128)(2,1)}, bf16[2,256,2,128]{3,1,2,0:T(8,128)(2,1)S(1)}, u32[]{:S(2)}, u32[]{:S(2)}) collective-permute-start(bf16[2,256,2,128]{3,1,2,0:T(8,128)(2,1)} %get-tuple-element.259), channel_id=1, source_target_pairs={{0,1},{1,2},{2,3},{3,4},{4,5},{5,6},{6,7},{7,0},{8,9},{9,10},{10,1... | collective-permute-start | bytes 786440 | tf_op jit(solution)/shard_map/while/body/eval_jaxpr/ppermute | solution.py:92
  73.1 1.2 copy-start.1
  75.3 1.0 copy-start.2
  77.0 5.8 %collective-permute-start = (bf16[2,256,2,128]{3,1,2,0:T(8,128)(2,1)}, bf16[2,256,2,128]{3,1,2,0:T(8,128)(2,1)S(1)}, u32[]{:S(2)}, u32[]{:S(2)}) collective-permute-start(bf16[2,256,2,128]{3,1,2,0:T(8,128)(2,1)} %get-tuple-element.259), channel_id=1, source_target_pairs={{0,1},{1,2},{2,3},{3,4},{4,5},{5,6},{6,7},{7,0},{8,9},{9,10},{10,1... | collective-permute-start | bytes 786440 | tf_op jit(solution)/shard_map/while/body/eval_jaxpr/ppermute | solution.py:92
  82.8 1.2 copy-start.1
  84.9 1.0 copy-start.2
  86.6 5.8 %collective-permute-start = (bf16[2,256,2,128]{3,1,2,0:T(8,128)(2,1)}, bf16[2,256,2,128]{3,1,2,0:T(8,128)(2,1)S(1)}, u32[]{:S(2)}, u32[]{:S(2)}) collective-permute-start(bf16[2,256,2,128]{3,1,2,0:T(8,128)(2,1)} %get-tuple-element.259), channel_id=1, source_target_pairs={{0,1},{1,2},{2,3},{3,4},{4,5},{5,6},{6,7},{7,0},{8,9},{9,10},{10,1... | collective-permute-start | bytes 786440 | tf_op jit(solution)/shard_map/while/body/eval_jaxpr/ppermute | solution.py:92
  92.4 1.2 copy-start.1
  94.5 1.0 copy-start.2
  96.2 5.8 %collective-permute-start = (bf16[2,256,2,128]{3,1,2,0:T(8,128)(2,1)}, bf16[2,256,2,128]{3,1,2,0:T(8,128)(2,1)S(1)}, u32[]{:S(2)}, u32[]{:S(2)}) collective-permute-start(bf16[2,256,2,128]{3,1,2,0:T(8,128)(2,1)} %get-tuple-element.259), channel_id=1, source_target_pairs={{0,1},{1,2},{2,3},{3,4},{4,5},{5,6},{6,7},{7,0},{8,9},{9,10},{10,1... | collective-permute-start | bytes 786440 | tf_op jit(solution)/shard_map/while/body/eval_jaxpr/ppermute | solution.py:92
  109.7 0.9 copy-start.6
Sparse Core Ops, SparseCore 0:
  109.9 64.5 all-reduce.1
where the time goes:
time: 188 us; the launch traced here: 186 us
  waiting for transfers between devices  104 us (55%)
  matrix products  30.3 us (16%)
  local copies, waits for them, and re-layouts  21.2 us (11%)
  other arithmetic  16.6 us (9%)
  between operations  14.2 us (8%)
    psum x1, waiting for transfers between devices, output_sum(): attn_sum = lax.psum(part_sum, 'tp')  63.1 us
    ppermute x7, waiting for transfers between devices, shift_step(): kv_blk = lax.ppermute(kv_blk, 'cp', shift_pairs)  40.6 us
    dot_general x1, matrix products, project_heads(): jnp.dot(normed, w_query, preferred_element_type=jnp.float32)  8.67 us
    cond x30, local copies, waits for them, and re-layouts  8.02 us
    dot_general x1, matrix products, output_sum(): jnp.einsum('ngte,ngef->tf', attn_o, w_out_r, preferred_element_type=jnp.f...  7.03 us
    dot_general x6, matrix products, attend_block(): jnp.einsum('ohut,tof->ohuf', weights.astype(jnp.bfloat16), kv_blk[1], pre...  5.47 us
    convert_element_type x1, other arithmetic, output_sum(): (hidden.astype(jnp.float32) + attn_sum.astype(jnp.float32)).astype(jnp.bf...  4.99 us
    while x7, local copies, waits for them, and re-layouts  4.92 us
  transfers between devices with their start and end apart: 8, of which 8 were waited for; matrix products, arithmetic and copies ran while one was open for 1% of the time, Pallas kernels for 0%

commit v1 on v0

v1 whole, which is shorter than its diff:
```python
import math
import functools
import jax
import jax.numpy as jnp
from jax import lax
from jax.experimental import pallas as pl
from jax.experimental.pallas import tpu as pltpu
from jax.sharding import PartitionSpec as P

HEAD = 128
EPS = 1e-5
LOG_THETA = math.log(1000000.0)
EXP2_SCALE = math.log2(math.e) / math.sqrt(HEAD)
MESH = pl.DeviceIdType.MESH
F32 = jnp.float32
BF16 = jnp.bfloat16
DISTANCES = (1, 3, 2)


def block_kernel(tp_n, cp_n, x_hbm, pos_ref, freq_ref, gain_ref, wq_hbm, wk_hbm, wv_hbm, wo_hbm,
                 out_hbm, k_hbm, v_hbm,
                 x_v, h_v, wkv_v, wq_v, wo_v, cos_v, sin_v, q_v, kv_v, kvo_v, m_v, l_v, acc_v, o_v,
                 part_v, sbuf, rbuf, out_v,
                 x_sem, wkv_sem, wq_sem, wo_sem, cache_sem, out_sem,
                 kv_send, kv_recv, fwd_send, fwd_recv, sib_send, sib_recv,
                 rs_send, rs_recv, ag_send, ag_recv):
    rows, width = x_v.shape
    chips = cp_n // 2
    heads = q_v.shape[0]
    kv_heads = kv_v.shape[0] // 2
    group = heads // kv_heads
    half = rows // 2
    chunk = width // tp_n
    sub = chunk // 2
    ty = lax.axis_index('tp')
    c_me = lax.axis_index('cp')
    chip = c_me // 2
    core = lax.rem(c_me, 2)
    sibling = chip * 2 + (1 - core)

    x_copy = pltpu.make_async_copy(x_hbm, x_v, x_sem)
    x_copy.start()
    kvw = kv_heads * HEAD
    wkv_copies = [pltpu.make_async_copy(wk_hbm, wkv_v.at[:, pl.ds(0, kvw)], wkv_sem.at[0]),
                  pltpu.make_async_copy(wv_hbm, wkv_v.at[:, pl.ds(kvw, kvw)], wkv_sem.at[1])]
    for cp in wkv_copies:
        cp.start()
    qw = wq_v.shape[1] // 2
    wq_copies = [pltpu.make_async_copy(wq_hbm.at[:, pl.ds(j * qw, qw)], wq_v.at[:, pl.ds(j * qw, qw)], wq_sem.at[j]) for j in range(2)]
    for cp in wq_copies:
        cp.start()
    wo_copy = pltpu.make_async_copy(wo_hbm, wo_v, wo_sem)
    wo_copy.start()

    barrier = pltpu.get_barrier_semaphore()
    y_next = lax.rem(ty + 1, tp_n)
    y_prev = lax.rem(ty + tp_n - 1, tp_n)
    partners = [{'tp': y_next}, {'tp': y_prev}, {'cp': sibling}]
    for d in range(1, chips):
        partners.append({'cp': lax.rem(c_me + 2 * d, cp_n)})
    for dev in partners:
        pl.semaphore_signal(barrier, inc=1, device_id=dev, device_id_type=MESH)

    angles = freq_ref[...] * pos_ref[...].astype(F32)
    cos_t = jnp.cos(angles)
    sin_t = jnp.sin(angles)
    cos_v[...] = jnp.concatenate([cos_t, cos_t], axis=0).T
    sin_v[...] = jnp.concatenate([-sin_t, sin_t], axis=0).T

    x_copy.wait()
    strip = 32

    def norm_strip(i, carry):
        r = pl.ds(pl.multiple_of(i * strip, strip), strip)
        xf = x_v[r, :].astype(F32)
        inv = lax.rsqrt(jnp.mean(xf * xf, axis=-1, keepdims=True) + EPS)
        h_v[r, :] = (xf * inv * gain_ref[...].astype(F32)).astype(BF16)
        return carry
    lax.fori_loop(0, rows // strip, norm_strip, 0)

    def rope(t):
        return t * cos_v[...] + pltpu.roll(t, HEAD // 2, 1) * sin_v[...]

    for cp in wkv_copies:
        cp.wait()
    kv_f = jnp.dot(h_v[...], wkv_v[...], preferred_element_type=F32)
    own_rows = pl.ds(pl.multiple_of(c_me * rows, rows), rows)
    for i in range(kv_heads):
        k_h = rope(kv_f[:, i * HEAD:(i + 1) * HEAD]).astype(BF16)
        kv_v[i, own_rows, :] = k_h
        kvo_v[0, :, i * HEAD:(i + 1) * HEAD] = k_h
        v_h = kv_f[:, kvw + i * HEAD:kvw + (i + 1) * HEAD].astype(BF16)
        kv_v[kv_heads + i, own_rows, :] = v_h
        kvo_v[1, :, i * HEAD:(i + 1) * HEAD] = v_h

    pl.semaphore_wait(barrier, len(partners))

    def kv_rows(c):
        return pl.ds(pl.multiple_of(c * rows, rows), rows)

    def kv_copy(src_c, target_c, ssem, rsem):
        ref = kv_v.at[:, kv_rows(src_c), :]
        return pltpu.make_async_remote_copy(src_ref=ref, dst_ref=ref, send_sem=ssem, recv_sem=rsem,
                                            device_id={'cp': target_c}, device_id_type=MESH)

    @pl.when(core == 0)
    def _():
        kv_copy(c_me, sibling, sib_send, sib_recv).start()
    for d in DISTANCES:
        @pl.when(chip + d < chips)
        def _(d=d):
            kv_copy(c_me, lax.rem(c_me + 2 * d, cp_n), kv_send.at[d - 1], kv_recv.at[d - 1]).start()
    k_cache = pltpu.make_async_copy(kvo_v.at[0], k_hbm, cache_sem.at[0])
    v_cache = pltpu.make_async_copy(kvo_v.at[1], v_hbm, cache_sem.at[1])
    k_cache.start()
    v_cache.start()

    for j in range(2):
        wq_copies[j].wait()
        q_f = jnp.dot(h_v[...], wq_v[:, j * qw:(j + 1) * qw], preferred_element_type=F32)
        for i in range(qw // HEAD):
            q_v[j * (qw // HEAD) + i] = rope(q_f[:, i * HEAD:(i + 1) * HEAD]).astype(BF16)

    def fold(p):
        out = p[:, 0:HEAD]
        for i in range(1, p.shape[1] // HEAD):
            out = out + p[:, i * HEAD:(i + 1) * HEAD]
        return out

    def own_head(hd, carry):
        kh = hd // group
        s = lax.dot_general(q_v[hd], kv_v[kh, own_rows, :], (((1,), (1,)), ((), ())), preferred_element_type=F32)
        r_i = lax.broadcasted_iota(jnp.int32, s.shape, 0)
        c_i = lax.broadcasted_iota(jnp.int32, s.shape, 1)
        s = jnp.where(c_i <= r_i, s, -jnp.inf)
        m = jnp.max(s, axis=1, keepdims=True)
        p = jnp.exp2((s - m) * EXP2_SCALE)
        m_v[hd] = jnp.broadcast_to(m, (rows, HEAD))
        l_v[hd] = fold(p)
        acc_v[hd] = jnp.dot(p.astype(BF16), kv_v[kv_heads + kh, own_rows, :], preferred_element_type=F32)
        return carry
    lax.fori_loop(0, heads, own_head, 0)

    def attend(start, count):
        keys = pl.ds(pl.multiple_of(start, rows), count)

        def one_head(hd, carry):
            kh = hd // group
            s = lax.dot_general(q_v[hd], kv_v[kh, keys, :], (((1,), (1,)), ((), ())), preferred_element_type=F32)
            m_old = m_v[hd]
            m_new = jnp.maximum(m_old, jnp.max(s, axis=1, keepdims=True))
            alpha = jnp.exp2((m_old - m_new) * EXP2_SCALE)
            p = jnp.exp2((s - m_new[:, 0:1]) * EXP2_SCALE)
            m_v[hd] = m_new
            l_v[hd] = l_v[hd] * alpha + fold(p)
            acc_v[hd] = acc_v[hd] * alpha + jnp.dot(p.astype(BF16), kv_v[kv_heads + kh, keys, :], preferred_element_type=F32)
            return carry
        lax.fori_loop(0, heads, one_head, 0)

    @pl.when(core == 1)
    def _():
        kv_copy(sibling, c_me, sib_send, sib_recv).wait_recv()
        attend(sibling * rows, rows)

    for d in DISTANCES:
        @pl.when(chip >= d)
        def _(d=d):
            src = c_me - 2 * d
            kv_copy(src, c_me, kv_send.at[d - 1], kv_recv.at[d - 1]).wait_recv()
            fwd = kv_copy(src, sibling, fwd_send.at[d - 1], fwd_recv.at[d - 1])
            fwd.start()
            other = sibling - 2 * d
            kv_copy(other, c_me, fwd_send.at[d - 1], fwd_recv.at[d - 1]).wait_recv()
            attend((chip - d) * 2 * rows, 2 * rows)

    def finish_head(hd, carry):
        total = jnp.sum(l_v[hd], axis=1, keepdims=True)
        o_v[:, pl.ds(pl.multiple_of(hd * HEAD, HEAD), HEAD)] = (acc_v[hd] / total).astype(BF16)
        return carry
    lax.fori_loop(0, heads, finish_head, 0)

    wo_copy.wait()
    targets = (y_next, y_prev)
    dir_rows = (pl.ds(0, half), pl.ds(half, half))
    subs = (pl.ds(0, sub), pl.ds(sub, sub))

    def rs_copy(dr, s, u):
        return pltpu.make_async_remote_copy(
            src_ref=sbuf.at[dr, s, :, subs[u]], dst_ref=rbuf.at[dr, s, :, subs[u]],
            send_sem=rs_send.at[dr, s, u], recv_sem=rs_recv.at[dr, s, u],
            device_id={'tp': targets[dr]}, device_id_type=MESH)

    def ag_copy(dr, a, u, idx):
        ref = out_v.at[idx, dir_rows[dr], subs[u]]
        return pltpu.make_async_remote_copy(
            src_ref=ref, dst_ref=ref, send_sem=ag_send.at[dr, a, u], recv_sem=ag_recv.at[dr, a, u],
            device_id={'tp': targets[dr]}, device_id_type=MESH)

    order = (y_prev, y_next, lax.rem(ty + 2, tp_n), ty)
    for i in range(tp_n):
        cols = pl.ds(pl.multiple_of(order[i] * chunk, HEAD), chunk)
        part = jnp.dot(o_v[...], wo_v[:, cols], preferred_element_type=F32)
        part_v[i] = part
        if i < 2:
            sbuf[i, 0] = part[i * half:(i + 1) * half].astype(BF16)
            for u in range(2):
                rs_copy(i, 0, u).start()

    use = ((2, 1), (2, 0))
    for s in (1, 2):
        for u in range(2):
            for dr in range(2):
                rs_copy(dr, s - 1, u).wait_recv()
                got = rbuf[dr, s - 1, :, subs[u]].astype(F32)
                sbuf[dr, s, :, subs[u]] = (got + part_v[use[dr][s - 1], dir_rows[dr], subs[u]]).astype(BF16)
                rs_copy(dr, s, u).start()

    def out_copy(dr, a, u, idx):
        cols = pl.ds(pl.multiple_of(idx * chunk + u * sub, HEAD), sub)
        return pltpu.make_async_copy(out_v.at[idx, dir_rows[dr], subs[u]], out_hbm.at[dir_rows[dr], cols], out_sem.at[dr, a, u])

    for u in range(2):
        for dr in range(2):
            rs_copy(dr, 2, u).wait_recv()
            cols = pl.ds(pl.multiple_of(ty * chunk + u * sub, HEAD), sub)
            a_sum = rbuf[dr, 2, :, subs[u]].astype(F32) + part_v[3, dir_rows[dr], subs[u]]
            out_v[ty, dir_rows[dr], subs[u]] = (x_v[dir_rows[dr], cols].astype(F32) + a_sum).astype(BF16)
            ag_copy(dr, 0, u, ty).start()
            out_copy(dr, 0, u, ty).start()

    def held(dr, a):
        return lax.rem(ty + tp_n - a, tp_n) if dr == 0 else lax.rem(ty + a, tp_n)

    for a in range(1, tp_n):
        for u in range(2):
            for dr in range(2):
                idx = held(dr, a)
                ag_copy(dr, a - 1, u, idx).wait_recv()
                if a < tp_n - 1:
                    ag_copy(dr, a, u, idx).start()
                out_copy(dr, a, u, idx).start()

    for a in range(tp_n):
        for u in range(2):
            for dr in range(2):
                out_copy(dr, a, u, held(dr, a)).wait()
                if a < tp_n - 1:
                    rs_copy(dr, a, u).wait_send()
                    ag_copy(dr, a, u, held(dr, a)).wait_send()
    k_cache.wait()
    v_cache.wait()

    @pl.when(core == 0)
    def _():
        kv_copy(c_me, sibling, sib_send, sib_recv).wait_send()
    for d in DISTANCES:
        @pl.when(chip + d < chips)
        def _(d=d):
            kv_copy(c_me, lax.rem(c_me + 2 * d, cp_n), kv_send.at[d - 1], kv_recv.at[d - 1]).wait_send()

        @pl.when(chip >= d)
        def _(d=d):
            kv_copy(c_me - 2 * d, sibling, fwd_send.at[d - 1], fwd_recv.at[d - 1]).wait_send()


def solution(mesh):
    tp_n = mesh.shape['tp']
    cp_n = mesh.shape['cp']
    row_spec = P(('dp', 'cp'), None)
    cache_spec = P(('dp', 'cp'), 'tp', None)
    head_cols = P(None, 'tp')

    def local_block(hidden, positions, norm_gain, w_query, w_key, w_value, w_out):
        rows, width = hidden.shape
        q_cols = w_query.shape[1]
        kv_cols = w_key.shape[1]
        heads = q_cols // HEAD
        kv_heads = kv_cols // HEAD
        chunk = width // tp_n
        half = rows // 2
        inv_freq = jnp.exp(jnp.arange(HEAD // 2, dtype=F32) * (-2.0 * LOG_THETA / HEAD))
        any_spec = pl.BlockSpec(memory_space=pl.ANY)
        vmem_spec = pl.BlockSpec(memory_space=pltpu.VMEM)
        dma = pltpu.SemaphoreType.DMA
        out, k_flat, v_flat = pl.pallas_call(
            functools.partial(block_kernel, tp_n, cp_n),
            out_shape=(jax.ShapeDtypeStruct((rows, width), BF16),
                       jax.ShapeDtypeStruct((rows, kv_cols), BF16),
                       jax.ShapeDtypeStruct((rows, kv_cols), BF16)),
            in_specs=[any_spec, vmem_spec, vmem_spec, vmem_spec, any_spec, any_spec, any_spec, any_spec],
            out_specs=(any_spec, any_spec, any_spec),
            scratch_shapes=[
                pltpu.VMEM((rows, width), BF16),
                pltpu.VMEM((rows, width), BF16),
                pltpu.VMEM((width, 2 * kv_cols), BF16),
                pltpu.VMEM((width, q_cols), BF16),
                pltpu.VMEM((q_cols, width), BF16),
                pltpu.VMEM((rows, HEAD), F32),
                pltpu.VMEM((rows, HEAD), F32),
                pltpu.VMEM((heads, rows, HEAD), BF16),
                pltpu.VMEM((2 * kv_heads, cp_n * rows, HEAD), BF16),
                pltpu.VMEM((2, rows, kv_cols), BF16),
                pltpu.VMEM((heads, rows, HEAD), F32),
                pltpu.VMEM((heads, rows, HEAD), F32),
                pltpu.VMEM((heads, rows, HEAD), F32),
                pltpu.VMEM((rows, q_cols), BF16),
                pltpu.VMEM((tp_n, rows, chunk), F32),
                pltpu.VMEM((2, tp_n - 1, half, chunk), BF16),
                pltpu.VMEM((2, tp_n - 1, half, chunk), BF16),
                pltpu.VMEM((tp_n, rows, chunk), BF16),
                dma, dma((2,)), dma((2,)), dma, dma((2,)), dma((2, tp_n, 2)),
                dma((3,)), dma((3,)), dma((3,)), dma((3,)), dma, dma,
                dma((2, tp_n - 1, 2)), dma((2, tp_n - 1, 2)), dma((2, tp_n - 1, 2)), dma((2, tp_n - 1, 2)),
            ],
            compiler_params=pltpu.CompilerParams(collective_id=0, has_side_effects=True, vmem_limit_bytes=64 * 1024 * 1024 - 65536),
        )(hidden, positions.reshape(1, rows), inv_freq.reshape(HEAD // 2, 1), norm_gain.reshape(1, width), w_query, w_key, w_value, w_out)
        return out, k_flat.reshape(rows, kv_heads, HEAD), v_flat.reshape(rows, kv_heads, HEAD)

    return jax.shard_map(local_block, mesh=mesh, in_specs=(row_spec, P(('dp', 'cp')), P(None), head_cols, head_cols, head_cols, P('tp', None)), out_specs=(row_spec, cache_spec, cache_spec), check_vma=False)
```

time: 188 us -> 96.1 us (0.51)
  waiting for transfers between devices: 104 us -> 0 us
  Pallas kernels: 0 us -> 86.6 us
  matrix products: 30.3 us -> 0 us
  other arithmetic: 16.6 us -> 0.64 us
  between operations: 14.2 us -> 0.64 us
  local copies, waits for them, and re-layouts: 21.2 us -> 7.91 us
    pallas_call x0 -> x1, Pallas kernels: none -> 86.6 us  [local_block(): pl.pallas_call(functools.partial(block_kernel, tp_n, cp_n), out_shape=(ja...]
    psum x1 -> x0, waiting for transfers between devices: 63.1 us -> none  [output_sum(): attn_sum = lax.psum(part_sum, 'tp')]
    ppermute x7 -> x0, waiting for transfers between devices: 40.6 us -> none  [shift_step(): kv_blk = lax.ppermute(kv_blk, 'cp', shift_pairs)]
    dot_general x18 -> x0, matrix products: 30.3 us -> none  [the longest x1 8.67 us: project_heads(): jnp.dot(normed, w_query, preferred_element_type=jnp.float32)]
    cond x30 -> x0, local copies, waits for them, and re-layouts: 8.02 us -> none
    convert_element_type x3 -> x0, other arithmetic: 6.53 us -> none  [the longest x1 4.99 us: output_sum(): (hidden.astype(jnp.float32) + attn_sum.astype(jnp.float32)).astype(jnp.bf...]
    while x7 -> x0, local copies, waits for them, and re-layouts: 4.92 us -> none
    reduce_sum x8 -> x0, other arithmetic: 4.87 us -> none  [the longest x1 2.34 us: rms_norm(): jnp.mean(hidden_f * hidden_f, axis=-1, keepdims=True) + EPS]
  transfers between devices with their start and end apart: 8 -> 0, of which waited for: 8 -> 0; matrix products, arithmetic and copies ran while one was open for 1% -> 0% of each run, Pallas kernels for 0% -> 0%
where the time goes in v1:
time: 96.1 us; the launch traced here: 95.8 us
  Pallas kernels  86.6 us (90%)
  local copies, waits for them, and re-layouts  7.91 us (8%)
    pallas_call x1, Pallas kernels, local_block(): pl.pallas_call(functools.partial(block_kernel, tp_n, cp_n), out_shape=(ja...  86.6 us
    unnamed x1, local copies, waits for them, and re-layouts  3.4 us

profile of v1, /device:TPU:102, one launch (start us, length us, event | category | flops | bytes accessed | tf_op | source)
XLA Modules:
  0.0 95.8 jit_solution(10171071269438536229)
XLA Ops:
  0.6 1.3 %reshape.30.gain_ref = bf16[1,5120]{1,0:T(2,128)(2,1)} reshape(bf16[5120]{0:T(1024)(128)(2,1)} %param.9) | data formatting | bytes 20480 | tf_op jit(solution)/shard_map/reshape | solution.py:316
  2.0 0.6 multiply_exponential_fusion.freq_ref
  2.6 86.6 %shard_map.94 = (bf16[256,5120]{1,0:T(8,128)(2,1)}, bf16[256,256]{1,0:T(8,128)(2,1)}, bf16[256,256]{1,0:T(8,128)(2,1)}) custom-call(bf16[256,5120]{1,0:T(8,128)(2,1)} %x_hbm.1, s32[1,256]{1,0:T(1,128)} %bitcast.1, f32[64,1]{1,0:T(8,128)} %multiply_exponential_fusion.freq_ref, bf16[1,5120]{1,0:T(2,128)(2,1)} %reshape.30.gain_ref, bf16[5120,1024]{1,0:T(8,128)(2,1)} %wq_hbm.1, ...), custom_call_target="tpu_custom_call" | custom-call | tf_op jit(solution)/shard_map/pallas_call | solution.py:285
  89.2 1.6 %reshape.31 = bf16[256,2,128]{2,1,0:T(2,128)(2,1)} reshape(bf16[256,256]{1,0:T(8,128)(2,1)} %get-tuple-element.7) | data formatting | bytes 262144 | tf_op jit(solution)/shard_map/reshape | solution.py:317
  90.8 1.6 %reshape.32 = bf16[256,2,128]{2,1,0:T(2,128)(2,1)} reshape(bf16[256,256]{1,0:T(8,128)(2,1)} %get-tuple-element.8) | data formatting | bytes 262144 | tf_op jit(solution)/shard_map/reshape | solution.py:317
  92.4 3.4 %copy.11 = bf16[256,5120]{1,0:T(8,128)(2,1)} copy(bf16[256,5120]{1,0:T(8,128)(2,1)} %get-tuple-element.12) | data formatting | bytes 5242880

commit v2 on v1

v2 whole, which is shorter than its diff:
```python
import math
import functools
import jax
import jax.numpy as jnp
from jax import lax
from jax.experimental import pallas as pl
from jax.experimental.pallas import tpu as pltpu
from jax.sharding import PartitionSpec as P

HEAD = 128
EPS = 1e-5
LOG_THETA = math.log(1000000.0)
EXP2_SCALE = math.log2(math.e) / math.sqrt(HEAD)
MESH = pl.DeviceIdType.MESH
F32 = jnp.float32
BF16 = jnp.bfloat16
UNROLL = 4
VMEM_LIMIT = 56 * 1024 * 1024


def block_kernel(tp_n, cp_n, x_hbm, pos_ref, gain_ref, wq_hbm, wk_hbm, wv_hbm, wo_hbm,
                 out_v, k_out, v_out,
                 x_v, h_v, wkv_v, wq_v, wo_v, gain_v, cos_v, sin_v, q_v, kv_v, m_v, l_v, acc_v, o_v,
                 part_v, sbuf, rbuf,
                 x_sem, wkv_sem, wq_sem, wo_sem,
                 own_send, relay_send, fwd_send, kv_recv, fwd_recv,
                 rs_send, rs_recv, ag_send, ag_recv):
    rows, width = x_v.shape
    chips = cp_n // 2
    heads = q_v.shape[0]
    kv_heads = kv_v.shape[0]
    group = heads // kv_heads
    half = rows // 2
    chunk = width // tp_n
    sub = chunk // 2
    ty = lax.axis_index('tp')
    c_me = lax.axis_index('cp')
    chip = c_me // 2
    core = lax.rem(c_me, 2)
    sibling = chip * 2 + (1 - core)

    x_copy = pltpu.make_async_copy(x_hbm, x_v, x_sem)
    x_copy.start()
    kvw = kv_heads * HEAD
    wkv_copies = [pltpu.make_async_copy(wk_hbm, wkv_v.at[:, pl.ds(0, kvw)], wkv_sem.at[0]),
                  pltpu.make_async_copy(wv_hbm, wkv_v.at[:, pl.ds(kvw, kvw)], wkv_sem.at[1])]
    for cp in wkv_copies:
        cp.start()
    qw = wq_v.shape[1] // 2
    wq_copies = [pltpu.make_async_copy(wq_hbm.at[:, pl.ds(j * qw, qw)], wq_v.at[:, pl.ds(j * qw, qw)], wq_sem.at[j]) for j in range(2)]
    wo_copy = pltpu.make_async_copy(wo_hbm, wo_v, wo_sem)

    barrier = pltpu.get_barrier_semaphore()
    y_next = lax.rem(ty + 1, tp_n)
    y_prev = lax.rem(ty + tp_n - 1, tp_n)
    partners = [{'tp': y_next}, {'tp': y_prev}, {'cp': sibling}]
    for d in range(1, chips):
        partners.append({'cp': lax.rem(c_me + 2 * d, cp_n)})
    for dev in partners:
        pl.semaphore_signal(barrier, inc=1, device_id=dev, device_id_type=MESH)

    freq = jnp.exp(lax.broadcasted_iota(jnp.int32, (HEAD // 2, rows), 0).astype(F32) * (-2.0 * LOG_THETA / HEAD))
    angles = pos_ref[...].astype(F32) * freq
    cos_t = jnp.cos(angles)
    sin_t = jnp.sin(angles)
    cos_v[...] = jnp.concatenate([cos_t, cos_t], axis=0).T
    sin_v[...] = jnp.concatenate([-sin_t, sin_t], axis=0).T

    gain_f = gain_ref[...].astype(F32)
    for i in range(width // HEAD):
        gain_v[:, i * HEAD:(i + 1) * HEAD] = gain_f[i:i + 1, :]

    x_copy.wait()
    for cp in wq_copies:
        cp.start()
    strip = 32

    def norm_strip(i, carry):
        r = pl.ds(pl.multiple_of(i * strip, strip), strip)
        xf = x_v[r, :].astype(F32)
        inv = lax.rsqrt(jnp.mean(xf * xf, axis=-1, keepdims=True) + EPS)
        h_v[r, :] = (xf * inv * gain_v[...]).astype(BF16)
        return carry
    lax.fori_loop(0, rows // strip, norm_strip, 0)

    def rope(t):
        return t * cos_v[...] + pltpu.roll(t, HEAD // 2, 1) * sin_v[...]

    for cp in wkv_copies:
        cp.wait()
    kv_f = jnp.dot(h_v[...], wkv_v[...], preferred_element_type=F32)
    wo_copy.start()

    def kv_rows(c):
        return pl.ds(pl.multiple_of(c * rows, rows), rows)

    own_rows = kv_rows(c_me)
    for i in range(kv_heads):
        k_h = rope(kv_f[:, i * HEAD:(i + 1) * HEAD]).astype(BF16)
        kv_v[i, 0, own_rows, :] = k_h
        v_h = kv_f[:, kvw + i * HEAD:kvw + (i + 1) * HEAD].astype(BF16)
        kv_v[i, 1, own_rows, :] = v_h

    pl.semaphore_wait(barrier, len(partners))

    def kv_copy(h, src_c, target_c, ssem, rsem):
        ref = kv_v.at[h, :, kv_rows(src_c), :]
        return pltpu.make_async_remote_copy(src_ref=ref, dst_ref=ref, send_sem=ssem, recv_sem=rsem,
                                            device_id={'cp': target_c}, device_id_type=MESH)

    def at_chip(i):
        return i * 2 + core

    plan = ((0, 3, (0, 1), 0), (0, 1, (0, 1), 1), (1, 0, (1,), 0), (1, 2, (0, 1), 1), (2, 3, (0, 1), 1))

    def own_copy(to, h, slot):
        return kv_copy(h, c_me, at_chip(to), own_send.at[slot, h], kv_recv.at[chip, h])

    def sib_copy(h):
        return kv_copy(h, c_me, sibling, fwd_send.at[chip, h], fwd_recv.at[chip, h])

    for frm in range(chips):
        @pl.when(chip == frm)
        def _(frm=frm):
            for h in range(kv_heads):
                for a, to, hs, slot in plan:
                    if a == frm and h in hs:
                        own_copy(to, h, slot).start()

    @pl.when(core == 0)
    def _():
        for h in range(kv_heads):
            sib_copy(h).start()

    for j in range(2):
        wq_copies[j].wait()
        q_f = jnp.dot(h_v[...], wq_v[:, j * qw:(j + 1) * qw], preferred_element_type=F32)
        for i in range(qw // HEAD):
            q_v[j * (qw // HEAD) + i] = rope(q_f[:, i * HEAD:(i + 1) * HEAD]).astype(BF16)

    def fold(p):
        out = p[:, 0:HEAD]
        for i in range(1, p.shape[1] // HEAD):
            out = out + p[:, i * HEAD:(i + 1) * HEAD]
        return out

    def scores(hd, kh, keys):
        return lax.dot_general(q_v[hd], kv_v[kh, 0, keys, :], (((1,), (1,)), ((), ())), preferred_element_type=F32)

    def own_heads(i, carry):
        hds = [i * UNROLL + u for u in range(UNROLL)]
        kh = hds[0] // group
        ss = [scores(hd, kh, own_rows) for hd in hds]
        r_i = lax.broadcasted_iota(jnp.int32, (rows, rows), 0)
        c_i = lax.broadcasted_iota(jnp.int32, (rows, rows), 1)
        ss = [jnp.where(c_i <= r_i, s, -jnp.inf) for s in ss]
        ms = [jnp.max(s, axis=1, keepdims=True) for s in ss]
        ps = [jnp.exp2((s - m) * EXP2_SCALE) for s, m in zip(ss, ms)]
        vals = kv_v[kh, 1, own_rows, :]
        accs = [jnp.dot(p.astype(BF16), vals, preferred_element_type=F32) for p in ps]
        for hd, m, p, acc in zip(hds, ms, ps, accs):
            m_v[hd] = jnp.broadcast_to(m, (rows, HEAD))
            l_v[hd] = fold(p)
            acc_v[hd] = acc
        return carry
    lax.fori_loop(0, heads // UNROLL, own_heads, 0)

    def attend(start, count):
        keys = pl.ds(pl.multiple_of(start, rows), count)

        def some_heads(i, carry):
            hds = [i * UNROLL + u for u in range(UNROLL)]
            kh = hds[0] // group
            ss = [scores(hd, kh, keys) for hd in hds]
            olds = [m_v[hd] for hd in hds]
            ls = [l_v[hd] for hd in hds]
            accs = [acc_v[hd] for hd in hds]
            news = [jnp.maximum(m, jnp.max(s, axis=1, keepdims=True)) for m, s in zip(olds, ss)]
            alphas = [jnp.exp2((m - n) * EXP2_SCALE) for m, n in zip(olds, news)]
            ps = [jnp.exp2((s - n[:, 0:1]) * EXP2_SCALE) for s, n in zip(ss, news)]
            vals = kv_v[kh, 1, keys, :]
            pvs = [jnp.dot(p.astype(BF16), vals, preferred_element_type=F32) for p in ps]
            for hd, n, l, a, p, acc, pv in zip(hds, news, ls, alphas, ps, accs, pvs):
                m_v[hd] = n
                l_v[hd] = l * a + fold(p)
                acc_v[hd] = acc * a + pv
            return carry
        lax.fori_loop(0, heads // UNROLL, some_heads, 0)

    def sib_wait(i, h):
        kv_copy(h, 2 * i + 1 - core, c_me, fwd_send.at[i, h], fwd_recv.at[i, h]).wait_recv()

    @pl.when(chip == 0)
    def _():
        kv_copy(1, at_chip(1), c_me, relay_send.at[0], kv_recv.at[1, 1]).wait_recv()
        kv_copy(1, at_chip(1), at_chip(3), relay_send.at[0], kv_recv.at[1, 1]).start()

    @pl.when(core == 1)
    def _():
        for h in range(kv_heads):
            sib_wait(chip, h)
        attend(sibling * rows, rows)

    for t in range(chips - 1):
        @pl.when(t < chip)
        def _(t=t):
            src = lax.rem(chip - 1 + chip // 3 - t + 3, 3)
            for h in range(kv_heads):
                kv_copy(h, at_chip(src), c_me, own_send.at[0, h], kv_recv.at[src, h]).wait_recv()
                if t == 0:
                    @pl.when(chip == 3)
                    def _():
                        kv_copy(h, at_chip(0), at_chip(2), relay_send.at[h], kv_recv.at[0, h]).start()
                    if h == 0:
                        @pl.when(chip == 2)
                        def _():
                            kv_copy(h, at_chip(1), at_chip(3), relay_send.at[0], kv_recv.at[1, h]).start()
                kv_copy(h, at_chip(src), sibling, fwd_send.at[src, h], fwd_recv.at[src, h]).start()
            for h in range(kv_heads):
                sib_wait(src, h)
            attend(src * 2 * rows, 2 * rows)

    def finish_head(hd, carry):
        total = jnp.sum(l_v[hd], axis=1, keepdims=True)
        o_v[:, pl.ds(pl.multiple_of(hd * HEAD, HEAD), HEAD)] = (acc_v[hd] / total).astype(BF16)
        return carry
    lax.fori_loop(0, heads, finish_head, 0)

    wo_copy.wait()
    targets = (y_next, y_prev)
    dir_rows = (pl.ds(0, half), pl.ds(half, half))
    subs = (pl.ds(0, sub), pl.ds(sub, sub))

    def rs_copy(dr, s, u):
        return pltpu.make_async_remote_copy(
            src_ref=sbuf.at[dr, s, :, subs[u]], dst_ref=rbuf.at[dr, s, :, subs[u]],
            send_sem=rs_send.at[dr, s, u], recv_sem=rs_recv.at[dr, s, u],
            device_id={'tp': targets[dr]}, device_id_type=MESH)

    def ag_copy(dr, a, u, idx):
        ref = out_v.at[dir_rows[dr], pl.ds(pl.multiple_of(idx * chunk + u * sub, HEAD), sub)]
        return pltpu.make_async_remote_copy(
            src_ref=ref, dst_ref=ref, send_sem=ag_send.at[dr, a, u], recv_sem=ag_recv.at[dr, a, u],
            device_id={'tp': targets[dr]}, device_id_type=MESH)

    order = (y_prev, y_next, lax.rem(ty + 2, tp_n), ty)
    for i in range(tp_n):
        cols = pl.ds(pl.multiple_of(order[i] * chunk, HEAD), chunk)
        part = jnp.dot(o_v[...], wo_v[:, cols], preferred_element_type=F32)
        part_v[i] = part
        if i < 2:
            sbuf[i, 0] = part[i * half:(i + 1) * half].astype(BF16)
            for u in range(2):
                rs_copy(i, 0, u).start()

    use = ((2, 1), (2, 0))
    for s in (1, 2):
        for u in range(2):
            for dr in range(2):
                rs_copy(dr, s - 1, u).wait_recv()
                got = rbuf[dr, s - 1, :, subs[u]].astype(F32)
                sbuf[dr, s, :, subs[u]] = (got + part_v[use[dr][s - 1], dir_rows[dr], subs[u]]).astype(BF16)
                rs_copy(dr, s, u).start()

    for u in range(2):
        for dr in range(2):
            rs_copy(dr, 2, u).wait_recv()
            cols = pl.ds(pl.multiple_of(ty * chunk + u * sub, HEAD), sub)
            a_sum = rbuf[dr, 2, :, subs[u]].astype(F32) + part_v[3, dir_rows[dr], subs[u]]
            out_v[dir_rows[dr], cols] = (x_v[dir_rows[dr], cols].astype(F32) + a_sum).astype(BF16)
            ag_copy(dr, 0, u, ty).start()

    def held(dr, a):
        return lax.rem(ty + tp_n - a, tp_n) if dr == 0 else lax.rem(ty + a, tp_n)

    for a in range(1, tp_n):
        for u in range(2):
            for dr in range(2):
                idx = held(dr, a)
                ag_copy(dr, a - 1, u, idx).wait_recv()
                if a < tp_n - 1:
                    ag_copy(dr, a, u, idx).start()

    k_out[...] = jnp.stack([kv_v[i, 0, own_rows, :] for i in range(kv_heads)], axis=1)
    v_out[...] = jnp.stack([kv_v[i, 1, own_rows, :] for i in range(kv_heads)], axis=1)

    for a in range(tp_n - 1):
        for u in range(2):
            for dr in range(2):
                rs_copy(dr, a, u).wait_send()
                ag_copy(dr, a, u, held(dr, a)).wait_send()
    for frm in range(chips):
        @pl.when(chip == frm)
        def _(frm=frm):
            for h in range(kv_heads):
                for a, to, hs, slot in plan:
                    if a == frm and h in hs:
                        own_copy(to, h, slot).wait_send()

    @pl.when(core == 0)
    def _():
        for h in range(kv_heads):
            sib_copy(h).wait_send()

    @pl.when(chip == 0)
    def _():
        kv_copy(1, at_chip(1), at_chip(3), relay_send.at[0], kv_recv.at[1, 1]).wait_send()

    @pl.when(chip == 2)
    def _():
        kv_copy(0, at_chip(1), at_chip(3), relay_send.at[0], kv_recv.at[1, 0]).wait_send()

    @pl.when(chip == 3)
    def _():
        for h in range(kv_heads):
            kv_copy(h, at_chip(0), at_chip(2), relay_send.at[h], kv_recv.at[0, h]).wait_send()
    for t in range(chips - 1):
        @pl.when(t < chip)
        def _(t=t):
            for h in range(kv_heads):
                kv_copy(h, at_chip(t), sibling, fwd_send.at[t, h], fwd_recv.at[t, h]).wait_send()


def solution(mesh):
    tp_n = mesh.shape['tp']
    cp_n = mesh.shape['cp']
    row_spec = P(('dp', 'cp'), None)
    cache_spec = P(('dp', 'cp'), 'tp', None)
    head_cols = P(None, 'tp')

    def local_block(hidden, positions, norm_gain, w_query, w_key, w_value, w_out):
        rows, width = hidden.shape
        q_cols = w_query.shape[1]
        kv_cols = w_key.shape[1]
        heads = q_cols // HEAD
        kv_heads = kv_cols // HEAD
        chunk = width // tp_n
        half = rows // 2
        any_spec = pl.BlockSpec(memory_space=pl.ANY)
        vmem_spec = pl.BlockSpec(memory_space=pltpu.VMEM)
        dma = pltpu.SemaphoreType.DMA
        chips = cp_n // 2
        out, k_cache, v_cache = pl.pallas_call(
            functools.partial(block_kernel, tp_n, cp_n),
            out_shape=(pltpu.VMEM((rows, width), BF16),
                       pltpu.VMEM((rows, kv_heads, HEAD), BF16),
                       pltpu.VMEM((rows, kv_heads, HEAD), BF16)),
            in_specs=[any_spec, vmem_spec, vmem_spec, any_spec, any_spec, any_spec, any_spec],
            out_specs=(vmem_spec, vmem_spec, vmem_spec),
            scratch_shapes=[
                pltpu.VMEM((rows, width), BF16),
                pltpu.VMEM((rows, width), BF16),
                pltpu.VMEM((width, 2 * kv_cols), BF16),
                pltpu.VMEM((width, q_cols), BF16),
                pltpu.VMEM((q_cols, width), BF16),
                pltpu.VMEM((1, width), F32),
                pltpu.VMEM((rows, HEAD), F32),
                pltpu.VMEM((rows, HEAD), F32),
                pltpu.VMEM((heads, rows, HEAD), BF16),
                pltpu.VMEM((kv_heads, 2, cp_n * rows, HEAD), BF16),
                pltpu.VMEM((heads, rows, HEAD), F32),
                pltpu.VMEM((heads, rows, HEAD), F32),
                pltpu.VMEM((heads, rows, HEAD), F32),
                pltpu.VMEM((rows, q_cols), BF16),
                pltpu.VMEM((tp_n, rows, chunk), F32),
                pltpu.VMEM((2, tp_n - 1, half, chunk), BF16),
                pltpu.VMEM((2, tp_n - 1, half, chunk), BF16),
                dma, dma((2,)), dma((2,)), dma,
                dma((2, kv_heads)), dma((kv_heads,)), dma((chips, kv_heads)), dma((chips, kv_heads)), dma((chips, kv_heads)),
                dma((2, tp_n - 1, 2)), dma((2, tp_n - 1, 2)), dma((2, tp_n - 1, 2)), dma((2, tp_n - 1, 2)),
            ],
            compiler_params=pltpu.CompilerParams(collective_id=0, has_side_effects=True, vmem_limit_bytes=VMEM_LIMIT),
        )(hidden, positions.reshape(1, rows), norm_gain.reshape(width // HEAD, HEAD), w_query, w_key, w_value, w_out)
        return out, k_cache, v_cache

    return jax.shard_map(local_block, mesh=mesh, in_specs=(row_spec, P(('dp', 'cp')), P(None), head_cols, head_cols, head_cols, P('tp', None)), out_specs=(row_spec, cache_spec, cache_spec), check_vma=False)
```

time: 96.1 us -> 79.5 us (0.83)
  Pallas kernels: 86.6 us -> 75.6 us
  local copies, waits for them, and re-layouts: 7.91 us -> 2.8 us
    pallas_call x1, Pallas kernels: 86.6 us -> 75.6 us  [local_block(): pl.pallas_call(functools.partial(block_kernel, tp_n, cp_n), out_shape=(pl...]
    reshape x3 -> x0, local copies, waits for them, and re-layouts: 4.51 us -> none  [the longest x1 1.6 us: local_block(): k_flat.reshape(rows, kv_heads, HEAD)]
    unnamed x1 -> x3, local copies, waits for them, and re-layouts: 3.4 us -> 2.8 us
where the time goes in v2:
time: 79.5 us; the launch traced here: 79.1 us
  Pallas kernels  75.6 us (95%)
  local copies, waits for them, and re-layouts  2.8 us (4%)
    pallas_call x1, Pallas kernels, local_block(): pl.pallas_call(functools.partial(block_kernel, tp_n, cp_n), out_shape=(pl...  75.6 us
    unnamed x3, local copies, waits for them, and re-layouts  2.8 us

profile of v2, /device:TPU:102, one launch (start us, length us, event | category | flops | bytes accessed | tf_op | source)
XLA Modules:
  0.0 79.1 jit_solution(17314540325210676498)
XLA Ops:
  0.6 75.6 %shard_map.94 = (bf16[256,5120]{1,0:T(8,128)(2,1)S(1)}, bf16[256,2,128]{2,1,0:T(2,128)(2,1)S(1)}, bf16[256,2,128]{2,1,0:T(2,128)(2,1)S(1)}) custom-call(bf16[256,5120]{1,0:T(8,128)(2,1)} %x_hbm.1, s32[1,256]{1,0:T(1,128)} %bitcast.3, bf16[40,128]{1,0:T(8,128)(2,1)} %bitcast.2, bf16[5120,1024]{1,0:T(8,128)(2,1)} %wq_hbm.1, bf16[5120,256]{1,0:T(8,128)(2,1)} %wk_hbm.1, ...), custom_call_target="tpu_custom_call" | custom-call | tf_op jit(solution)/shard_map/pallas_call | solution.py:343
  76.3 1.5 %copy.13 = bf16[256,5120]{1,0:T(8,128)(2,1)} copy(bf16[256,5120]{1,0:T(8,128)(2,1)S(1)} %get-tuple-element.3) | data formatting | bytes 5242880
  77.8 0.7 copy.14
  78.4 0.7 copy.15

commit v3 on v2

--- a/solution.py
+++ b/solution.py
@@ -15,13 +15,17 @@
 F32 = jnp.float32
 BF16 = jnp.bfloat16
 UNROLL = 4
+X_STRIPS = 4
+KV_STRIPS = 2
+Q_STRIPS = 2
+NORM_ROWS = 64
 VMEM_LIMIT = 56 * 1024 * 1024
 
 
 def block_kernel(tp_n, cp_n, x_hbm, pos_ref, gain_ref, wq_hbm, wk_hbm, wv_hbm, wo_hbm,
                  out_v, k_out, v_out,
                  x_v, h_v, wkv_v, wq_v, wo_v, gain_v, cos_v, sin_v, q_v, kv_v, m_v, l_v, acc_v, o_v,
-                 part_v, sbuf, rbuf,
+                 part_v, sbuf, rbuf, kv_acc,
                  x_sem, wkv_sem, wq_sem, wo_sem,
                  own_send, relay_send, fwd_send, kv_recv, fwd_recv,
                  rs_send, rs_recv, ag_send, ag_recv):
@@ -39,16 +43,22 @@
     core = lax.rem(c_me, 2)
     sibling = chip * 2 + (1 - core)
 
-    x_copy = pltpu.make_async_copy(x_hbm, x_v, x_sem)
-    x_copy.start()
+    strip = rows // X_STRIPS
+    depth = width // KV_STRIPS
     kvw = kv_heads * HEAD
-    wkv_copies = [pltpu.make_async_copy(wk_hbm, wkv_v.at[:, pl.ds(0, kvw)], wkv_sem.at[0]),
-                  pltpu.make_async_copy(wv_hbm, wkv_v.at[:, pl.ds(kvw, kvw)], wkv_sem.at[1])]
-    for cp in wkv_copies:
+    qw = wq_v.shape[1] // Q_STRIPS
+    x_copies = [pltpu.make_async_copy(x_hbm.at[pl.ds(i * strip, strip)], x_v.at[pl.ds(i * strip, strip)], x_sem.at[i])
+                for i in range(X_STRIPS)]
+    wkv_copies = [[pltpu.make_async_copy(w_hbm.at[pl.ds(i * depth, depth)],
+                                         wkv_v.at[pl.ds(i * depth, depth), pl.ds(n * kvw, kvw)], wkv_sem.at[n, i])
+                   for n, w_hbm in enumerate((wk_hbm, wv_hbm))] for i in range(KV_STRIPS)]
+    wq_copies = [pltpu.make_async_copy(wq_hbm.at[:, pl.ds(j * qw, qw)], wq_v.at[:, pl.ds(j * qw, qw)], wq_sem.at[j])
+                 for j in range(Q_STRIPS)]
+    wo_copy = pltpu.make_async_copy(wo_hbm, wo_v, wo_sem)
+    for cp in x_copies:
         cp.start()
-    qw = wq_v.shape[1] // 2
-    wq_copies = [pltpu.make_async_copy(wq_hbm.at[:, pl.ds(j * qw, qw)], wq_v.at[:, pl.ds(j * qw, qw)], wq_sem.at[j]) for j in range(2)]
-    wo_copy = pltpu.make_async_copy(wo_hbm, wo_v, wo_sem)
+    for cp in wkv_copies[0]:
+        cp.start()
 
     barrier = pltpu.get_barrier_semaphore()
     y_next = lax.rem(ty + 1, tp_n)
@@ -70,26 +80,36 @@
     for i in range(width // HEAD):
         gain_v[:, i * HEAD:(i + 1) * HEAD] = gain_f[i:i + 1, :]
 
-    x_copy.wait()
-    for cp in wq_copies:
-        cp.start()
-    strip = 32
-
-    def norm_strip(i, carry):
-        r = pl.ds(pl.multiple_of(i * strip, strip), strip)
-        xf = x_v[r, :].astype(F32)
-        inv = lax.rsqrt(jnp.mean(xf * xf, axis=-1, keepdims=True) + EPS)
-        h_v[r, :] = (xf * inv * gain_v[...]).astype(BF16)
-        return carry
-    lax.fori_loop(0, rows // strip, norm_strip, 0)
+    for i in range(X_STRIPS):
+        x_copies[i].wait()
+
+        def norm_rows(n, carry, i=i):
+            r = pl.ds(pl.multiple_of(i * strip + n * NORM_ROWS, NORM_ROWS), NORM_ROWS)
+            xf = x_v[r, :].astype(F32)
+            inv = lax.rsqrt(jnp.mean(xf * xf, axis=-1, keepdims=True) + EPS)
+            h_v[r, :] = (xf * inv * gain_v[...]).astype(BF16)
+            return carry
+        lax.fori_loop(0, strip // NORM_ROWS, norm_rows, 0)
+        if i == 0:
+            for pair in wkv_copies[1:]:
+                for cp in pair:
+                    cp.start()
+        if i == X_STRIPS - 1:
+            for cp in wq_copies:
+                cp.start()
 
     def rope(t):
         return t * cos_v[...] + pltpu.roll(t, HEAD // 2, 1) * sin_v[...]
 
-    for cp in wkv_copies:
-        cp.wait()
-    kv_f = jnp.dot(h_v[...], wkv_v[...], preferred_element_type=F32)
-    wo_copy.start()
+    for i in range(KV_STRIPS):
+        for cp in wkv_copies[i]:
+            cp.wait()
+        part_kv = jnp.dot(h_v[:, i * depth:(i + 1) * depth], wkv_v[i * depth:(i + 1) * depth, :], preferred_element_type=F32)
+        if i == 0:
+            kv_acc[...] = part_kv
+        else:
+            kv_acc[...] += part_kv
+    kv_f = kv_acc[...]
 
     def kv_rows(c):
         return pl.ds(pl.multiple_of(c * rows, rows), rows)
@@ -132,8 +152,10 @@
         for h in range(kv_heads):
             sib_copy(h).start()
 
-    for j in range(2):
+    for j in range(Q_STRIPS):
         wq_copies[j].wait()
+        if j == Q_STRIPS - 1:
+            wo_copy.start()
         q_f = jnp.dot(h_v[...], wq_v[:, j * qw:(j + 1) * qw], preferred_element_type=F32)
         for i in range(qw // HEAD):
             q_v[j * (qw // HEAD) + i] = rope(q_f[:, i * HEAD:(i + 1) * HEAD]).astype(BF16)
@@ -165,12 +187,11 @@
         return carry
     lax.fori_loop(0, heads // UNROLL, own_heads, 0)
 
-    def attend(start, count):
+    def attend(start, count, kh):
         keys = pl.ds(pl.multiple_of(start, rows), count)
 
         def some_heads(i, carry):
-            hds = [i * UNROLL + u for u in range(UNROLL)]
-            kh = hds[0] // group
+            hds = [kh * group + i * UNROLL + u for u in range(UNROLL)]
             ss = [scores(hd, kh, keys) for hd in hds]
             olds = [m_v[hd] for hd in hds]
             ls = [l_v[hd] for hd in hds]
@@ -185,7 +206,7 @@
                 l_v[hd] = l * a + fold(p)
                 acc_v[hd] = acc * a + pv
             return carry
-        lax.fori_loop(0, heads // UNROLL, some_heads, 0)
+        lax.fori_loop(0, group // UNROLL, some_heads, 0)
 
     def sib_wait(i, h):
         kv_copy(h, 2 * i + 1 - core, c_me, fwd_send.at[i, h], fwd_recv.at[i, h]).wait_recv()
@@ -199,26 +220,61 @@
     def _():
         for h in range(kv_heads):
             sib_wait(chip, h)
-        attend(sibling * rows, rows)
-
-    for t in range(chips - 1):
-        @pl.when(t < chip)
-        def _(t=t):
-            src = lax.rem(chip - 1 + chip // 3 - t + 3, 3)
-            for h in range(kv_heads):
-                kv_copy(h, at_chip(src), c_me, own_send.at[0, h], kv_recv.at[src, h]).wait_recv()
-                if t == 0:
-                    @pl.when(chip == 3)
-                    def _():
-                        kv_copy(h, at_chip(0), at_chip(2), relay_send.at[h], kv_recv.at[0, h]).start()
-                    if h == 0:
-                        @pl.when(chip == 2)
-                        def _():
-                            kv_copy(h, at_chip(1), at_chip(3), relay_send.at[0], kv_recv.at[1, h]).start()
-                kv_copy(h, at_chip(src), sibling, fwd_send.at[src, h], fwd_recv.at[src, h]).start()
-            for h in range(kv_heads):
-                sib_wait(src, h)
-            attend(src * 2 * rows, 2 * rows)
+            attend(sibling * rows, rows, h)
+
+    def source(t):
+        return lax.rem(chip - 1 + chip // 3 - t + 3, 3)
+
+    def take(t, h):
+        src = source(t)
+        kv_copy(h, at_chip(src), c_me, own_send.at[0, h], kv_recv.at[src, h]).wait_recv()
+        if t == 0:
+            @pl.when(chip == 1)
+            def _():
+                kv_copy(h, at_chip(0), at_chip(2), relay_send.at[h], kv_recv.at[0, h]).start()
+            if h == 0:
+                @pl.when(chip == 2)
+                def _():
+                    kv_copy(h, at_chip(1), at_chip(3), relay_send.at[0], kv_recv.at[1, h]).start()
+        kv_copy(h, at_chip(src), sibling, fwd_send.at[src, h], fwd_recv.at[src, h]).start()
+
+    def use_block(t, h):
+        src = source(t)
+        sib_wait(src, h)
+        attend(src * 2 * rows, 2 * rows, h)
+
+    @pl.when(chip == 3)
+    def _():
+        take(0, 0)
+        take(1, 0)
+        use_block(0, 0)
+        take(0, 1)
+        take(1, 1)
+        use_block(1, 0)
+        use_block(0, 1)
+        take(2, 0)
+        take(2, 1)
+        use_block(1, 1)
+        use_block(2, 0)
+        use_block(2, 1)
+
+    @pl.when((chip == 1) | (chip == 2))
+    def _():
+        take(0, 0)
+        take(0, 1)
+        use_block(0, 0)
+
+    @pl.when(chip == 1)
+    def _():
+        use_block(0, 1)
+
+    @pl.when(chip == 2)
+    def _():
+        take(1, 0)
+        use_block(0, 1)
+        take(1, 1)
+        use_block(1, 0)
+        use_block(1, 1)
 
     def finish_head(hd, carry):
         total = jnp.sum(l_v[hd], axis=1, keepdims=True)
@@ -244,14 +300,20 @@
             device_id={'tp': targets[dr]}, device_id_type=MESH)
 
     order = (y_prev, y_next, lax.rem(ty + 2, tp_n), ty)
-    for i in range(tp_n):
+    def project(i, r):
         cols = pl.ds(pl.multiple_of(order[i] * chunk, HEAD), chunk)
-        part = jnp.dot(o_v[...], wo_v[:, cols], preferred_element_type=F32)
-        part_v[i] = part
-        if i < 2:
-            sbuf[i, 0] = part[i * half:(i + 1) * half].astype(BF16)
-            for u in range(2):
-                rs_copy(i, 0, u).start()
+        return jnp.dot(o_v[r, :], wo_v[:, cols], preferred_element_type=F32)
+
+    for dr in range(2):
+        sbuf[dr, 0] = project(dr, dir_rows[dr]).astype(BF16)
+        for u in range(2):
+            rs_copy(dr, 0, u).start()
+    for i in (2, 0, 1, 3):
+        r = pl.ds(0, rows) if i > 1 else dir_rows[1 - i]
+        part_v[i, r, :] = project(i, r)
+
+    k_out[...] = jnp.stack([kv_v[i, 0, own_rows, :] for i in range(kv_heads)], axis=1)
+    v_out[...] = jnp.stack([kv_v[i, 1, own_rows, :] for i in range(kv_heads)], axis=1)
 
     use = ((2, 1), (2, 0))
     for s in (1, 2):
@@ -280,9 +342,6 @@
                 ag_copy(dr, a - 1, u, idx).wait_recv()
                 if a < tp_n - 1:
                     ag_copy(dr, a, u, idx).start()
-
-    k_out[...] = jnp.stack([kv_v[i, 0, own_rows, :] for i in range(kv_heads)], axis=1)
-    v_out[...] = jnp.stack([kv_v[i, 1, own_rows, :] for i in range(kv_heads)], axis=1)
 
     for a in range(tp_n - 1):
         for u in range(2):
@@ -310,7 +369,7 @@
     def _():
         kv_copy(0, at_chip(1), at_chip(3), relay_send.at[0], kv_recv.at[1, 0]).wait_send()
 
-    @pl.when(chip == 3)
+    @pl.when(chip == 1)
     def _():
         for h in range(kv_heads):
             kv_copy(h, at_chip(0), at_chip(2), relay_send.at[h], kv_recv.at[0, h]).wait_send()
@@ -319,6 +378,15 @@
         def _(t=t):
             for h in range(kv_heads):
                 kv_copy(h, at_chip(t), sibling, fwd_send.at[t, h], fwd_recv.at[t, h]).wait_send()
+
+
+def store_kernel(out_v, k_v, v_v, out_hbm, k_hbm, v_hbm, sem):
+    pairs = ((k_v, k_hbm), (v_v, v_hbm), (out_v, out_hbm))
+    copies = [pltpu.make_async_copy(src, dst, sem.at[i]) for i, (src, dst) in enumerate(pairs)]
+    for cp in copies:
+        cp.start()
+    for cp in copies:
+        cp.wait()
 
 
 def solution(mesh):
@@ -365,12 +433,20 @@
                 pltpu.VMEM((tp_n, rows, chunk), F32),
                 pltpu.VMEM((2, tp_n - 1, half, chunk), BF16),
                 pltpu.VMEM((2, tp_n - 1, half, chunk), BF16),
-                dma, dma((2,)), dma((2,)), dma,
+                pltpu.VMEM((rows, 2 * kv_cols), F32),
+                dma((X_STRIPS,)), dma((2, KV_STRIPS)), dma((Q_STRIPS,)), dma,
                 dma((2, kv_heads)), dma((kv_heads,)), dma((chips, kv_heads)), dma((chips, kv_heads)), dma((chips, kv_heads)),
                 dma((2, tp_n - 1, 2)), dma((2, tp_n - 1, 2)), dma((2, tp_n - 1, 2)), dma((2, tp_n - 1, 2)),
             ],
             compiler_params=pltpu.CompilerParams(collective_id=0, has_side_effects=True, vmem_limit_bytes=VMEM_LIMIT),
         )(hidden, positions.reshape(1, rows), norm_gain.reshape(width // HEAD, HEAD), w_query, w_key, w_value, w_out)
-        return out, k_cache, v_cache
+        results = (out, k_cache, v_cache)
+        return pl.pallas_call(
+            store_kernel,
+            out_shape=tuple(jax.ShapeDtypeStruct(r.shape, BF16) for r in results),
+            in_specs=[vmem_spec] * 3,
+            out_specs=(any_spec,) * 3,
+            scratch_shapes=[dma((3,))],
+        )(*[pltpu.with_memory_space_constraint(r, pltpu.VMEM) for r in results])
 
     return jax.shard_map(local_block, mesh=mesh, in_specs=(row_spec, P(('dp', 'cp')), P(None), head_cols, head_cols, head_cols, P('tp', None)), out_specs=(row_spec, cache_spec, cache_spec), check_vma=False)

time: 79.5 us -> 73.5 us (0.925)
  Pallas kernels: 75.6 us -> 72.5 us
  local copies, waits for them, and re-layouts: 2.8 us -> 0 us
    pallas_call x1, Pallas kernels: 75.6 us -> 70.9 us  [local_block(): pl.pallas_call(functools.partial(block_kernel, tp_n, cp_n), out_shape=(pl...]
    unnamed x3 -> x0, local copies, waits for them, and re-layouts: 2.8 us -> none
    pallas_call x0 -> x1, Pallas kernels: none -> 1.61 us  [local_block(): pl.pallas_call(store_kernel, out_shape=tuple((jax.ShapeDtypeStruct(r.shap...]
where the time goes in v3:
time: 73.5 us; the launch traced here: 73.4 us
  Pallas kernels  72.5 us (99%)
  between operations  0.82 us (1%)
    pallas_call x1, Pallas kernels, local_block(): pl.pallas_call(functools.partial(block_kernel, tp_n, cp_n), out_shape=(pl...  70.9 us
    pallas_call x1, Pallas kernels, local_block(): pl.pallas_call(store_kernel, out_shape=tuple((jax.ShapeDtypeStruct(r.shap...  1.61 us

profile of v3, /device:TPU:102, one launch (start us, length us, event | category | flops | bytes accessed | tf_op | source)
XLA Modules:
  0.0 73.4 jit_solution(2524837680823884141)
XLA Ops:
  0.6 70.9 %shard_map.94 = (bf16[256,5120]{1,0:T(8,128)(2,1)S(1)}, bf16[256,2,128]{2,1,0:T(2,128)(2,1)S(1)}, bf16[256,2,128]{2,1,0:T(2,128)(2,1)S(1)}) custom-call(bf16[256,5120]{1,0:T(8,128)(2,1)} %x_hbm.1, s32[1,256]{1,0:T(1,128)} %bitcast.3, bf16[40,128]{1,0:T(8,128)(2,1)} %bitcast.2, bf16[5120,1024]{1,0:T(8,128)(2,1)} %wq_hbm.1, bf16[5120,256]{1,0:T(8,128)(2,1)} %wk_hbm.1, ...), custom_call_target="tpu_custom_call" | custom-call | tf_op jit(solution)/shard_map/pallas_call | solution.py:411
  71.6 1.6 %shard_map.95 = (bf16[256,5120]{1,0:T(8,128)(2,1)}, bf16[256,2,128]{2,1,0:T(2,128)(2,1)}, bf16[256,2,128]{2,1,0:T(2,128)(2,1)}) custom-call(bf16[256,5120]{1,0:T(8,128)(2,1)S(1)} %get-tuple-element.6.out_v, bf16[256,2,128]{2,1,0:T(2,128)(2,1)S(1)} %get-tuple-element.7.k_v, bf16[256,2,128]{2,1,0:T(2,128)(2,1)S(1)} %get-tuple-element.8.v_v), custom_call_target="tpu_custom_call" | custom-call | tf_op jit(solution)/shard_map/pallas_call | solution.py:444

commit v4 on v3

--- a/solution.py
+++ b/solution.py
@@ -14,7 +14,7 @@
 MESH = pl.DeviceIdType.MESH
 F32 = jnp.float32
 BF16 = jnp.bfloat16
-UNROLL = 4
+MERGE = 4
 X_STRIPS = 4
 KV_STRIPS = 2
 Q_STRIPS = 2
@@ -131,7 +131,7 @@
     def at_chip(i):
         return i * 2 + core
 
-    plan = ((0, 3, (0, 1), 0), (0, 1, (0, 1), 1), (1, 0, (1,), 0), (1, 2, (0, 1), 1), (2, 3, (0, 1), 1))
+    plan = ((0, 3, 1, 0), (0, 1, 0, 1), (0, 3, 0, 0), (0, 1, 1, 1), (1, 0, 1, 0), (1, 2, 0, 1), (1, 2, 1, 1), (2, 3, 1, 1), (2, 3, 0, 1))
 
     def own_copy(to, h, slot):
         return kv_copy(h, c_me, at_chip(to), own_send.at[slot, h], kv_recv.at[chip, h])
@@ -142,10 +142,9 @@
     for frm in range(chips):
         @pl.when(chip == frm)
         def _(frm=frm):
-            for h in range(kv_heads):
-                for a, to, hs, slot in plan:
-                    if a == frm and h in hs:
-                        own_copy(to, h, slot).start()
+            for a, to, h, slot in plan:
+                if a == frm:
+                    own_copy(to, h, slot).start()
 
     @pl.when(core == 0)
     def _():
@@ -160,53 +159,55 @@
         for i in range(qw // HEAD):
             q_v[j * (qw // HEAD) + i] = rope(q_f[:, i * HEAD:(i + 1) * HEAD]).astype(BF16)
 
-    def fold(p):
-        out = p[:, 0:HEAD]
-        for i in range(1, p.shape[1] // HEAD):
-            out = out + p[:, i * HEAD:(i + 1) * HEAD]
-        return out
+    span = MERGE * rows
+
+    def merged(ref, hd):
+        return ref[pl.ds(hd, MERGE)].reshape(span, HEAD)
+
+    def put(ref, hd, val):
+        ref[pl.ds(hd, MERGE)] = val.reshape(MERGE, rows, HEAD)
+
+    def tiles(s):
+        return [s[:, i * HEAD:(i + 1) * HEAD] for i in range(s.shape[1] // HEAD)]
 
     def scores(hd, kh, keys):
-        return lax.dot_general(q_v[hd], kv_v[kh, 0, keys, :], (((1,), (1,)), ((), ())), preferred_element_type=F32)
+        return lax.dot_general(merged(q_v, hd), kv_v[kh, 0, keys, :], (((1,), (1,)), ((), ())), preferred_element_type=F32)
+
+    def row_max(s):
+        return jnp.broadcast_to(jnp.max(functools.reduce(jnp.maximum, tiles(s)), axis=1, keepdims=True), (span, HEAD))
 
     def own_heads(i, carry):
-        hds = [i * UNROLL + u for u in range(UNROLL)]
-        kh = hds[0] // group
-        ss = [scores(hd, kh, own_rows) for hd in hds]
-        r_i = lax.broadcasted_iota(jnp.int32, (rows, rows), 0)
-        c_i = lax.broadcasted_iota(jnp.int32, (rows, rows), 1)
-        ss = [jnp.where(c_i <= r_i, s, -jnp.inf) for s in ss]
-        ms = [jnp.max(s, axis=1, keepdims=True) for s in ss]
-        ps = [jnp.exp2((s - m) * EXP2_SCALE) for s, m in zip(ss, ms)]
-        vals = kv_v[kh, 1, own_rows, :]
-        accs = [jnp.dot(p.astype(BF16), vals, preferred_element_type=F32) for p in ps]
-        for hd, m, p, acc in zip(hds, ms, ps, accs):
-            m_v[hd] = jnp.broadcast_to(m, (rows, HEAD))
-            l_v[hd] = fold(p)
-            acc_v[hd] = acc
+        hd = i * MERGE
+        kh = hd // group
+        s = scores(hd, kh, own_rows)
+        r_i = lax.rem(lax.broadcasted_iota(jnp.int32, (span, rows), 0), rows)
+        c_i = lax.broadcasted_iota(jnp.int32, (span, rows), 1)
+        s = jnp.where(c_i <= r_i, s, -jnp.inf)
+        m = row_max(s)
+        ps = [jnp.exp2((t - m) * EXP2_SCALE) for t in tiles(s)]
+        p = jnp.concatenate([t.astype(BF16) for t in ps], axis=1)
+        put(m_v, hd, m)
+        put(l_v, hd, functools.reduce(jnp.add, ps))
+        put(acc_v, hd, jnp.dot(p, kv_v[kh, 1, own_rows, :], preferred_element_type=F32))
         return carry
-    lax.fori_loop(0, heads // UNROLL, own_heads, 0)
+    lax.fori_loop(0, heads // MERGE, own_heads, 0)
 
     def attend(start, count, kh):
         keys = pl.ds(pl.multiple_of(start, rows), count)
 
         def some_heads(i, carry):
-            hds = [kh * group + i * UNROLL + u for u in range(UNROLL)]
-            ss = [scores(hd, kh, keys) for hd in hds]
-            olds = [m_v[hd] for hd in hds]
-            ls = [l_v[hd] for hd in hds]
-            accs = [acc_v[hd] for hd in hds]
-            news = [jnp.maximum(m, jnp.max(s, axis=1, keepdims=True)) for m, s in zip(olds, ss)]
-            alphas = [jnp.exp2((m - n) * EXP2_SCALE) for m, n in zip(olds, news)]
-            ps = [jnp.exp2((s - n[:, 0:1]) * EXP2_SCALE) for s, n in zip(ss, news)]
-            vals = kv_v[kh, 1, keys, :]
-            pvs = [jnp.dot(p.astype(BF16), vals, preferred_element_type=F32) for p in ps]
-            for hd, n, l, a, p, acc, pv in zip(hds, news, ls, alphas, ps, accs, pvs):
-                m_v[hd] = n
-                l_v[hd] = l * a + fold(p)
-                acc_v[hd] = acc * a + pv
+            hd = kh * group + i * MERGE
+            s = scores(hd, kh, keys)
+            old = merged(m_v, hd)
+            new = jnp.maximum(old, row_max(s))
+            alpha = jnp.exp2((old - new) * EXP2_SCALE)
+            ps = [jnp.exp2((t - new) * EXP2_SCALE) for t in tiles(s)]
+            p = jnp.concatenate([t.astype(BF16) for t in ps], axis=1)
+            put(m_v, hd, new)
+            put(l_v, hd, merged(l_v, hd) * alpha + functools.reduce(jnp.add, ps))
+            put(acc_v, hd, merged(acc_v, hd) * alpha + jnp.dot(p, kv_v[kh, 1, keys, :], preferred_element_type=F32))
             return carry
-        lax.fori_loop(0, group // UNROLL, some_heads, 0)
+        lax.fori_loop(0, group // MERGE, some_heads, 0)
 
     def sib_wait(i, h):
         kv_copy(h, 2 * i + 1 - core, c_me, fwd_send.at[i, h], fwd_recv.at[i, h]).wait_recv()
@@ -225,17 +226,19 @@
     def source(t):
         return lax.rem(chip - 1 + chip // 3 - t + 3, 3)
 
+    relays = ((1, 0, 2, 0), (3, 0, 2, 1), (2, 1, 3, 0))
+
+    def relay(a, frm, b, h):
+        return kv_copy(h, at_chip(frm), at_chip(b), relay_send.at[0], kv_recv.at[frm, h])
+
     def take(t, h):
         src = source(t)
         kv_copy(h, at_chip(src), c_me, own_send.at[0, h], kv_recv.at[src, h]).wait_recv()
-        if t == 0:
-            @pl.when(chip == 1)
-            def _():
-                kv_copy(h, at_chip(0), at_chip(2), relay_send.at[h], kv_recv.at[0, h]).start()
-            if h == 0:
-                @pl.when(chip == 2)
-                def _():
-                    kv_copy(h, at_chip(1), at_chip(3), relay_send.at[0], kv_recv.at[1, h]).start()
+        for a, frm, b, hh in relays:
+            if t == 0 and h == hh:
+                @pl.when(chip == a)
+                def _(a=a, frm=frm, b=b):
+                    relay(a, frm, b, h).start()
         kv_copy(h, at_chip(src), sibling, fwd_send.at[src, h], fwd_recv.at[src, h]).start()
 
     def use_block(t, h):
@@ -245,16 +248,16 @@
 
     @pl.when(chip == 3)
     def _():
+        take(0, 1)
+        take(1, 1)
+        use_block(0, 1)
         take(0, 0)
         take(1, 0)
+        use_block(1, 1)
         use_block(0, 0)
-        take(0, 1)
-        take(1, 1)
-        use_block(1, 0)
-        use_block(0, 1)
         take(2, 0)
         take(2, 1)
-        use_block(1, 1)
+        use_block(1, 0)
         use_block(2, 0)
         use_block(2, 1)
 
@@ -270,11 +273,11 @@
 
     @pl.when(chip == 2)
     def _():
-        take(1, 0)
         use_block(0, 1)
         take(1, 1)
+        take(1, 0)
+        use_block(1, 1)
         use_block(1, 0)
-        use_block(1, 1)
 
     def finish_head(hd, carry):
         total = jnp.sum(l_v[hd], axis=1, keepdims=True)
@@ -351,10 +354,9 @@
     for frm in range(chips):
         @pl.when(chip == frm)
         def _(frm=frm):
-            for h in range(kv_heads):
-                for a, to, hs, slot in plan:
-                    if a == frm and h in hs:
-                        own_copy(to, h, slot).wait_send()
+            for a, to, h, slot in plan:
+                if a == frm:
+                    own_copy(to, h, slot).wait_send()
 
     @pl.when(core == 0)
     def _():
@@ -365,14 +367,10 @@
     def _():
         kv_copy(1, at_chip(1), at_chip(3), relay_send.at[0], kv_recv.at[1, 1]).wait_send()
 
-    @pl.when(chip == 2)
-    def _():
-        kv_copy(0, at_chip(1), at_chip(3), relay_send.at[0], kv_recv.at[1, 0]).wait_send()
-
-    @pl.when(chip == 1)
-    def _():
-        for h in range(kv_heads):
-            kv_copy(h, at_chip(0), at_chip(2), relay_send.at[h], kv_recv.at[0, h]).wait_send()
+    for a, frm, b, h in relays:
+        @pl.when(chip == a)
+        def _(a=a, frm=frm, b=b, h=h):
+            relay(a, frm, b, h).wait_send()
     for t in range(chips - 1):
         @pl.when(t < chip)
         def _(t=t):
@@ -435,7 +433,7 @@
                 pltpu.VMEM((2, tp_n - 1, half, chunk), BF16),
                 pltpu.VMEM((rows, 2 * kv_cols), F32),
                 dma((X_STRIPS,)), dma((2, KV_STRIPS)), dma((Q_STRIPS,)), dma,
-                dma((2, kv_heads)), dma((kv_heads,)), dma((chips, kv_heads)), dma((chips, kv_heads)), dma((chips, kv_heads)),
+                dma((2, kv_heads)), dma((1,)), dma((chips, kv_heads)), dma((chips, kv_heads)), dma((chips, kv_heads)),
                 dma((2, tp_n - 1, 2)), dma((2, tp_n - 1, 2)), dma((2, tp_n - 1, 2)), dma((2, tp_n - 1, 2)),
             ],
             compiler_params=pltpu.CompilerParams(collective_id=0, has_side_effects=True, vmem_limit_bytes=VMEM_LIMIT),

time: 73.5 us -> 71.2 us (0.969)
  Pallas kernels: 72.5 us -> 70.2 us
    pallas_call x1, Pallas kernels: 70.9 us -> 68.6 us  [local_block(): pl.pallas_call(functools.partial(block_kernel, tp_n, cp_n), out_shape=(pl...]
where the time goes in v4:
time: 71.2 us; the launch traced here: 71 us
  Pallas kernels  70.2 us (99%)
  between operations  0.82 us (1%)
    pallas_call x1, Pallas kernels, local_block(): pl.pallas_call(functools.partial(block_kernel, tp_n, cp_n), out_shape=(pl...  68.6 us
    pallas_call x1, Pallas kernels, local_block(): pl.pallas_call(store_kernel, out_shape=tuple((jax.ShapeDtypeStruct(r.shap...  1.61 us

profile of v4, /device:TPU:102, one launch (start us, length us, event | category | flops | bytes accessed | tf_op | source)
XLA Modules:
  0.0 71.0 jit_solution(1155866284279168295)
XLA Ops:
  0.6 68.6 %shard_map.94 = (bf16[256,5120]{1,0:T(8,128)(2,1)S(1)}, bf16[256,2,128]{2,1,0:T(2,128)(2,1)S(1)}, bf16[256,2,128]{2,1,0:T(2,128)(2,1)S(1)}) custom-call(bf16[256,5120]{1,0:T(8,128)(2,1)} %x_hbm.1, s32[1,256]{1,0:T(1,128)} %bitcast.3, bf16[40,128]{1,0:T(8,128)(2,1)} %bitcast.2, bf16[5120,1024]{1,0:T(8,128)(2,1)} %wq_hbm.1, bf16[5120,256]{1,0:T(8,128)(2,1)} %wk_hbm.1, ...), custom_call_target="tpu_custom_call" | custom-call | tf_op jit(solution)/shard_map/pallas_call | solution.py:409
  69.2 1.6 %shard_map.95 = (bf16[256,5120]{1,0:T(8,128)(2,1)}, bf16[256,2,128]{2,1,0:T(2,128)(2,1)}, bf16[256,2,128]{2,1,0:T(2,128)(2,1)}) custom-call(bf16[256,5120]{1,0:T(8,128)(2,1)S(1)} %get-tuple-element.6.out_v, bf16[256,2,128]{2,1,0:T(2,128)(2,1)S(1)} %get-tuple-element.7.k_v, bf16[256,2,128]{2,1,0:T(2,128)(2,1)S(1)} %get-tuple-element.8.v_v), custom_call_target="tpu_custom_call" | custom-call | tf_op jit(solution)/shard_map/pallas_call | solution.py:442

commit v5 on v4

--- a/solution.py
+++ b/solution.py
@@ -36,7 +36,7 @@
     group = heads // kv_heads
     half = rows // 2
     chunk = width // tp_n
-    sub = chunk // 2
+    cut = chunk * 2 // 5
     ty = lax.axis_index('tp')
     c_me = lax.axis_index('cp')
     chip = c_me // 2
@@ -57,8 +57,9 @@
     wo_copy = pltpu.make_async_copy(wo_hbm, wo_v, wo_sem)
     for cp in x_copies:
         cp.start()
-    for cp in wkv_copies[0]:
-        cp.start()
+    for pair in wkv_copies[:1]:
+        for cp in pair:
+            cp.start()
 
     barrier = pltpu.get_barrier_semaphore()
     y_next = lax.rem(ty + 1, tp_n)
@@ -241,6 +242,14 @@
                     relay(a, frm, b, h).start()
         kv_copy(h, at_chip(src), sibling, fwd_send.at[src, h], fwd_recv.at[src, h]).start()
 
+    def use_direct(t, h):
+        attend((source(t) * 2 + core) * rows, rows, h)
+
+    def use_passed(t, h):
+        src = source(t)
+        sib_wait(src, h)
+        attend((src * 2 + 1 - core) * rows, rows, h)
+
     def use_block(t, h):
         src = source(t)
         sib_wait(src, h)
@@ -250,10 +259,12 @@
     def _():
         take(0, 1)
         take(1, 1)
-        use_block(0, 1)
+        use_direct(0, 1)
+        use_direct(1, 1)
+        use_passed(0, 1)
         take(0, 0)
         take(1, 0)
-        use_block(1, 1)
+        use_passed(1, 1)
         use_block(0, 0)
         take(2, 0)
         take(2, 1)
@@ -276,8 +287,10 @@
         use_block(0, 1)
         take(1, 1)
         take(1, 0)
-        use_block(1, 1)
-        use_block(1, 0)
+        use_direct(1, 1)
+        use_direct(1, 0)
+        use_passed(1, 1)
+        use_passed(1, 0)
 
     def finish_head(hd, carry):
         total = jnp.sum(l_v[hd], axis=1, keepdims=True)
@@ -288,7 +301,9 @@
     wo_copy.wait()
     targets = (y_next, y_prev)
     dir_rows = (pl.ds(0, half), pl.ds(half, half))
-    subs = (pl.ds(0, sub), pl.ds(sub, sub))
+    subs = (pl.ds(0, cut), pl.ds(cut, chunk - cut))
+    starts = (0, cut)
+    sizes = (cut, chunk - cut)
 
     def rs_copy(dr, s, u):
         return pltpu.make_async_remote_copy(
@@ -297,19 +312,19 @@
             device_id={'tp': targets[dr]}, device_id_type=MESH)
 
     def ag_copy(dr, a, u, idx):
-        ref = out_v.at[dir_rows[dr], pl.ds(pl.multiple_of(idx * chunk + u * sub, HEAD), sub)]
+        ref = out_v.at[dir_rows[dr], pl.ds(pl.multiple_of(idx * chunk + starts[u], HEAD), sizes[u])]
         return pltpu.make_async_remote_copy(
             src_ref=ref, dst_ref=ref, send_sem=ag_send.at[dr, a, u], recv_sem=ag_recv.at[dr, a, u],
             device_id={'tp': targets[dr]}, device_id_type=MESH)
 
     order = (y_prev, y_next, lax.rem(ty + 2, tp_n), ty)
-    def project(i, r):
-        cols = pl.ds(pl.multiple_of(order[i] * chunk, HEAD), chunk)
+    def project(i, r, first=0, size=chunk):
+        cols = pl.ds(pl.multiple_of(order[i] * chunk + first, HEAD), size)
         return jnp.dot(o_v[r, :], wo_v[:, cols], preferred_element_type=F32)
 
-    for dr in range(2):
-        sbuf[dr, 0] = project(dr, dir_rows[dr]).astype(BF16)
-        for u in range(2):
+    for u in range(2):
+        for dr in range(2):
+            sbuf[dr, 0, :, subs[u]] = project(dr, dir_rows[dr], starts[u], sizes[u]).astype(BF16)
             rs_copy(dr, 0, u).start()
     for i in (2, 0, 1, 3):
         r = pl.ds(0, rows) if i > 1 else dir_rows[1 - i]
@@ -330,7 +345,7 @@
     for u in range(2):
         for dr in range(2):
             rs_copy(dr, 2, u).wait_recv()
-            cols = pl.ds(pl.multiple_of(ty * chunk + u * sub, HEAD), sub)
+            cols = pl.ds(pl.multiple_of(ty * chunk + starts[u], HEAD), sizes[u])
             a_sum = rbuf[dr, 2, :, subs[u]].astype(F32) + part_v[3, dir_rows[dr], subs[u]]
             out_v[dir_rows[dr], cols] = (x_v[dir_rows[dr], cols].astype(F32) + a_sum).astype(BF16)
             ag_copy(dr, 0, u, ty).start()

time: 71.2 us -> 70.8 us (level)
  no operation moved by 1% of the time
where the time goes in v5:
time: 70.8 us; the launch traced here: 70.6 us
  Pallas kernels  69.8 us (99%)
  between operations  0.82 us (1%)
    pallas_call x1, Pallas kernels, local_block(): pl.pallas_call(functools.partial(block_kernel, tp_n, cp_n), out_shape=(pl...  68.2 us
    pallas_call x1, Pallas kernels, local_block(): pl.pallas_call(store_kernel, out_shape=tuple((jax.ShapeDtypeStruct(r.shap...  1.61 us

profile of v5, /device:TPU:102, one launch (start us, length us, event | category | flops | bytes accessed | tf_op | source)
XLA Modules:
  0.0 70.6 jit_solution(16208778622119865363)
XLA Ops:
  0.6 68.2 %shard_map.94 = (bf16[256,5120]{1,0:T(8,128)(2,1)S(1)}, bf16[256,2,128]{2,1,0:T(2,128)(2,1)S(1)}, bf16[256,2,128]{2,1,0:T(2,128)(2,1)S(1)}) custom-call(bf16[256,5120]{1,0:T(8,128)(2,1)} %x_hbm.1, s32[1,256]{1,0:T(1,128)} %bitcast.3, bf16[40,128]{1,0:T(8,128)(2,1)} %bitcast.2, bf16[5120,1024]{1,0:T(8,128)(2,1)} %wq_hbm.1, bf16[5120,256]{1,0:T(8,128)(2,1)} %wk_hbm.1, ...), custom_call_target="tpu_custom_call" | custom-call | tf_op jit(solution)/shard_map/pallas_call | solution.py:424
  68.8 1.6 %shard_map.95 = (bf16[256,5120]{1,0:T(8,128)(2,1)}, bf16[256,2,128]{2,1,0:T(2,128)(2,1)}, bf16[256,2,128]{2,1,0:T(2,128)(2,1)}) custom-call(bf16[256,5120]{1,0:T(8,128)(2,1)S(1)} %get-tuple-element.6.out_v, bf16[256,2,128]{2,1,0:T(2,128)(2,1)S(1)} %get-tuple-element.7.k_v, bf16[256,2,128]{2,1,0:T(2,128)(2,1)S(1)} %get-tuple-element.8.v_v), custom_call_target="tpu_custom_call" | custom-call | tf_op jit(solution)/shard_map/pallas_call | solution.py:457

commit v6 on v5

--- a/solution.py
+++ b/solution.py
@@ -191,7 +191,7 @@
         put(l_v, hd, functools.reduce(jnp.add, ps))
         put(acc_v, hd, jnp.dot(p, kv_v[kh, 1, own_rows, :], preferred_element_type=F32))
         return carry
-    lax.fori_loop(0, heads // MERGE, own_heads, 0)
+    lax.fori_loop(0, heads // MERGE, own_heads, 0, unroll=True)
 
     def attend(start, count, kh):
         keys = pl.ds(pl.multiple_of(start, rows), count)
@@ -296,7 +296,7 @@
         total = jnp.sum(l_v[hd], axis=1, keepdims=True)
         o_v[:, pl.ds(pl.multiple_of(hd * HEAD, HEAD), HEAD)] = (acc_v[hd] / total).astype(BF16)
         return carry
-    lax.fori_loop(0, heads, finish_head, 0)
+    lax.fori_loop(0, heads, finish_head, 0, unroll=True)
 
     wo_copy.wait()
     targets = (y_next, y_prev)

time: 70.8 us -> 69.7 us (0.984)
  Pallas kernels: 69.8 us -> 68.7 us
    pallas_call x1, Pallas kernels: 68.2 us -> 67.1 us  [local_block(): pl.pallas_call(functools.partial(block_kernel, tp_n, cp_n), out_shape=(pl...]
where the time goes in v6:
time: 69.7 us; the launch traced here: 69.5 us
  Pallas kernels  68.7 us (99%)
  between operations  0.82 us (1%)
    pallas_call x1, Pallas kernels, local_block(): pl.pallas_call(functools.partial(block_kernel, tp_n, cp_n), out_shape=(pl...  67.1 us
    pallas_call x1, Pallas kernels, local_block(): pl.pallas_call(store_kernel, out_shape=tuple((jax.ShapeDtypeStruct(r.shap...  1.61 us

profile of v6, /device:TPU:102, one launch (start us, length us, event | category | flops | bytes accessed | tf_op | source)
XLA Modules:
  0.0 69.5 jit_solution(14621121619210552957)
XLA Ops:
  0.6 67.1 %shard_map.94 = (bf16[256,5120]{1,0:T(8,128)(2,1)S(1)}, bf16[256,2,128]{2,1,0:T(2,128)(2,1)S(1)}, bf16[256,2,128]{2,1,0:T(2,128)(2,1)S(1)}) custom-call(bf16[256,5120]{1,0:T(8,128)(2,1)} %x_hbm.1, s32[1,256]{1,0:T(1,128)} %bitcast.3, bf16[40,128]{1,0:T(8,128)(2,1)} %bitcast.2, bf16[5120,1024]{1,0:T(8,128)(2,1)} %wq_hbm.1, bf16[5120,256]{1,0:T(8,128)(2,1)} %wk_hbm.1, ...), custom_call_target="tpu_custom_call" | custom-call | tf_op jit(solution)/shard_map/pallas_call | solution.py:424
  67.7 1.6 %shard_map.95 = (bf16[256,5120]{1,0:T(8,128)(2,1)}, bf16[256,2,128]{2,1,0:T(2,128)(2,1)}, bf16[256,2,128]{2,1,0:T(2,128)(2,1)}) custom-call(bf16[256,5120]{1,0:T(8,128)(2,1)S(1)} %get-tuple-element.6.out_v, bf16[256,2,128]{2,1,0:T(2,128)(2,1)S(1)} %get-tuple-element.7.k_v, bf16[256,2,128]{2,1,0:T(2,128)(2,1)S(1)} %get-tuple-element.8.v_v), custom_call_target="tpu_custom_call" | custom-call | tf_op jit(solution)/shard_map/pallas_call | solution.py:457
